TPU v7x, 128 devices: a whole 4x4x4 slice. The times are simulated.
128 devices in a mesh: gx: 4 (over x), gy: 32 (over y, z, core).
Axes of the slice: x: 4, y: 4, z: 4, core: 2. Of those that a mesh axis runs over, the one named last changes fastest.
Arguments:
- grid_latent: bfloat16 [65536, 512], P(('gx', 'gy')), may hold values from -6 to 6
- mesh_latent: bfloat16 [16384, 512], P(('gx', 'gy')), may hold values from -6 to 6
- encode_senders: int32 [32, 16384], P(None, ('gx', 'gy')), may hold values from -1 to 65535, as said below
- mesh_senders: int32 [32, 16384], P(None, ('gx', 'gy')), may hold values from -1 to 16383, as said below
- decode_senders: int32 [3, 65536], P(None, ('gx', 'gy')), may hold values from 0 to 16383, as said below
- encoder_edges: bfloat16 [3, 512, 512], replicated, may hold values from -0.25 to 0.25
- encoder_edgebias: float32 [2, 512], replicated, may hold values from -3 to 3
- encoder_nodes: bfloat16 [3, 512, 512], replicated, may hold values from -0.25 to 0.25
- encoder_nodebias: float32 [2, 512], replicated, may hold values from -3 to 3
- process_edges: bfloat16 [3, 512, 512], replicated, may hold values from -0.25 to 0.25
- process_edgebias: float32 [2, 512], replicated, may hold values from -3 to 3
- process_nodes: bfloat16 [3, 512, 512], replicated, may hold values from -0.25 to 0.25
- process_nodebias: float32 [2, 512], replicated, may hold values from -3 to 3
- decoder_edges: bfloat16 [3, 512, 512], replicated, may hold values from -0.25 to 0.25
- decoder_edgebias: float32 [2, 512], replicated, may hold values from -3 to 3
- decoder_nodes: bfloat16 [3, 512, 512], replicated, may hold values from -0.25 to 0.25
- decoder_nodebias: float32 [2, 512], replicated, may hold values from -3 to 3
Outputs:
- decoded_grid: bfloat16 [65536, 512], P(('gx', 'gy'))
- processed_mesh: bfloat16 [16384, 512], P(('gx', 'gy'))
Inputs may be any that keep to these rules, and one draw needn't show every extreme that they name: `encode_senders`: devices form a torus of regions, device number = gx index * gy size + gy index, and device d owns grid points d * 512 to (d + 1) * 512 - 1. In each column the live senders come first, then -1; a column has 8 to 32 live senders and some column has 32. A live sender is a grid point of the column's own device, or one of the first 128 grid points of one of the eight devices around it on the torus (wrapping on both axes). `mesh_senders`: device d owns mesh nodes d * 128 to (d + 1) * 128 - 1. In each column the live senders come first, then -1; a column has 8 to 32 live senders and some column has 32. A live sender is a mesh node of the column's own device, or one of the first 32 mesh nodes of one of the eight devices around it on the torus, or one of the first 4 mesh nodes of any device. `decode_senders`: every entry is live: a mesh node of the grid point's own device, or one of the first 32 mesh nodes of one of the eight devices around it on the torus.
All inputs are finite; a program needn't handle non-finite values.
Results may differ from a plain program's by a relative error of at most 0.013.
Values may be sent and summed in bfloat16 or wider, within the bound.
A program may use at most 64 MiB of HBM per device.

v0:
```python
import jax
import jax.numpy as jnp
from jax import lax
from jax.sharding import Mesh
from jax.sharding import PartitionSpec as P

CM = 4
GY = ("gy_0", "gy_1", "gy_2")
GX_GY = ("gx", "gy_0", "gy_1", "gy_2")


def with_halo(shard, sides, width):
    for axis, dim in sides:
        peers, length = (lax.axis_size(axis), shard.shape[dim])
        up = [(i, (i + 1) % peers) for i in range(peers)]
        down = [(j, i) for i, j in up]
        last = lax.slice_in_dim(shard, length - width, length, axis=dim)
        initial = lax.slice_in_dim(shard, 0, width, axis=dim)
        before = lax.ppermute(last, axis, up)
        after = lax.ppermute(initial, axis, down)
        shard = jnp.concatenate([before, shard, after], axis=dim)
    return shard


def from_everyone(shard, axis):
    copies = jnp.broadcast_to(shard, (lax.axis_size(axis), *shard.shape))
    return lax.all_to_all(copies, axis, split_axis=0, concat_axis=0, tiled=True)


def laid_out(tiles, dim):
    lengths = list(tiles.shape[1:])
    lengths[dim] *= tiles.shape[0]
    return jnp.moveaxis(tiles, 0, dim).reshape(lengths)


def gathered_by_axis(shard, axes, dim):
    far, near = axes
    tiles = from_everyone(from_everyone(shard, far), near)
    return laid_out(tiles.swapaxes(0, 1).reshape(-1, *shard.shape), dim)


def project(latent, weight):
    return jnp.dot(latent, weight, preferred_element_type=jnp.float32)


def finish(preact, weights, vectors):
    hidden = jax.nn.silu(preact).astype(jnp.bfloat16)
    output = jnp.dot(hidden, weights[2], preferred_element_type=jnp.float32)
    centre = jnp.mean(output, axis=-1, keepdims=True)
    centred = output - centre
    spread = jnp.mean(centred * centred, axis=-1, keepdims=True)
    return centred * lax.rsqrt(spread + 1e-05) * (1.0 + vectors[1])


def block_size(count, degree):
    target = max(1, 4096 // degree)
    chosen = min(count, target)
    while count % chosen:
        chosen -= 1
    return chosen


def aggregate(sources, receiving, positions, active, weights, vectors):
    degree, count = positions.shape
    chosen = block_size(count, degree)
    blocks = count // chosen
    source_rows, width = sources.shape
    shifted = (receiving + vectors[0]).reshape(blocks, chosen, width)
    places = positions.reshape(degree, blocks, chosen).transpose(1, 0, 2)
    masks = active.reshape(degree, blocks, chosen).transpose(1, 0, 2)
    columns = lax.broadcasted_iota(jnp.int32, (1, source_rows), 1)

    def one_block(item):
        base, place, present = item
        selector = (place.reshape(degree * chosen, 1) == columns).astype(jnp.bfloat16)
        picked = jnp.dot(selector, sources, preferred_element_type=jnp.float32).astype(jnp.bfloat16)
        preact = project(picked, weights[0]).reshape(degree, chosen, width) + base[None]
        message = finish(preact.reshape(degree * chosen, width), weights, vectors)
        message = message.reshape(degree, chosen, width)
        return jnp.sum(jnp.where(present[..., None], message, 0.0), axis=0)

    return lax.map(one_block, (shifted, places, masks)).reshape(count, width)


def update(latent, summed, weights, vectors):
    preact = (
        project(latent, weights[0]) + project(summed.astype(jnp.bfloat16), weights[1]) + vectors[0]
    )
    return (latent.astype(jnp.float32) + finish(preact, weights, vectors)).astype(jnp.bfloat16)


def locate(sender_ids, rows, border, coarse, place_x, place_y, size_x, size_y):
    cleaned = jnp.maximum(sender_ids, 0)
    owner = cleaned // rows
    offset = cleaned % rows
    owner_x = owner // size_y
    owner_y = owner % size_y
    step_x = (owner_x - place_x) % size_x
    step_y = (owner_y - place_y) % size_y
    slot_x = jnp.where(step_x == 1, 2, jnp.where(step_x == size_x - 1, 0, 1))
    slot_y = jnp.where(step_y == 1, 2, jnp.where(step_y == size_y - 1, 0, 1))
    nearby = (
        ((step_x <= 1) | (step_x == size_x - 1))
        & ((step_y <= 1) | (step_y == size_y - 1))
        & (offset < border)
    )
    itself = (step_x == 0) & (step_y == 0)
    rim_place = rows + (slot_x * 3 + slot_y) * border + offset
    far_place = rows + 9 * border + owner * coarse + offset
    return jnp.where(itself, offset, jnp.where(nearby, rim_place, far_place))


def per_device(
    grid_latent,
    mesh_latent,
    encode_senders,
    mesh_senders,
    decode_senders,
    encoder_edges,
    encoder_edgebias,
    encoder_nodes,
    encoder_nodebias,
    process_edges,
    process_edgebias,
    process_nodes,
    process_nodebias,
    decoder_edges,
    decoder_edgebias,
    decoder_nodes,
    decoder_nodebias,
):
    grid_rows, width = grid_latent.shape
    mesh_rows = mesh_latent.shape[0]
    grid_border = grid_rows // 4
    mesh_border = mesh_rows // 4
    size_x = lax.axis_size("gx")
    size_y = lax.axis_size(GY)
    place_x = lax.axis_index("gx")
    place_y = lax.axis_index(GY)
    border_rows = grid_latent[:grid_border].reshape(1, 1, grid_border, width)
    rim_rows = with_halo(border_rows, (("gx", 0), (GY, 1)), 1)
    grid_sources = jnp.concatenate([grid_latent, rim_rows.reshape(9 * grid_border, width)], axis=0)
    positions = locate(encode_senders, grid_rows, grid_border, 0, place_x, place_y, size_x, size_y)
    summed = aggregate(
        grid_sources,
        project(mesh_latent, encoder_edges[1]),
        positions,
        encode_senders >= 0,
        encoder_edges,
        encoder_edgebias,
    )
    encoded = update(mesh_latent, summed, encoder_nodes, encoder_nodebias)
    mesh_rim = with_halo(
        encoded[:mesh_border].reshape(1, 1, mesh_border, width), (("gx", 0), (GY, 1)), 1
    )
    coarse_rows = gathered_by_axis(encoded[:CM], (("gx", "gy_0", "gy_1"), "gy_2"), 0)
    mesh_sources = jnp.concatenate(
        [encoded, mesh_rim.reshape(9 * mesh_border, width), coarse_rows], axis=0
    )
    positions = locate(mesh_senders, mesh_rows, mesh_border, CM, place_x, place_y, size_x, size_y)
    summed = aggregate(
        mesh_sources,
        project(encoded, process_edges[1]),
        positions,
        mesh_senders >= 0,
        process_edges,
        process_edgebias,
    )
    processed = update(encoded, summed, process_nodes, process_nodebias)
    final_rim = with_halo(
        processed[:mesh_border].reshape(1, 1, mesh_border, width), (("gx", 0), (GY, 1)), 1
    )
    decode_sources = jnp.concatenate([processed, final_rim.reshape(9 * mesh_border, width)], axis=0)
    positions = locate(decode_senders, mesh_rows, mesh_border, 0, place_x, place_y, size_x, size_y)
    summed = aggregate(
        decode_sources,
        project(grid_latent, decoder_edges[1]),
        positions,
        decode_senders >= 0,
        decoder_edges,
        decoder_edgebias,
    )
    decoded = update(grid_latent, summed, decoder_nodes, decoder_nodebias)
    return (decoded, processed)


def solution(mesh):
    finer = Mesh(mesh.devices.reshape(mesh.shape["gx"], 4, 4, 2), ("gx", "gy_0", "gy_1", "gy_2"))
    placed = (
        P(GX_GY, None),
        P(GX_GY, None),
        P(None, GX_GY),
        P(None, GX_GY),
        P(None, GX_GY),
        P(),
        P(),
        P(),
        P(),
        P(),
        P(),
        P(),
        P(),
        P(),
        P(),
        P(),
        P(),
    )
    return jax.shard_map(
        per_device,
        mesh=finer,
        in_specs=placed,
        out_specs=(P(GX_GY, None), P(GX_GY, None)),
        check_vma=False,
    )
```

profile of v0, /device:TPU:0, one launch (start us, length us, event | category | flops | bytes accessed | tf_op | source)
XLA Modules:
  0.0 113.4 jit_solution(7733595736142119721)
XLA Ops:
  1.6 1.7 %collective-permute-start = (bf16[1,1,128,512]{3,2,1,0:T(8,128)(2,1)S(1)}, bf16[1,1,128,512]{3,2,1,0:T(8,128)(2,1)S(1)}, u32[]{:S(2)}, u32[]{:S(2)}) collective-permute-start(bf16[1,1,128,512]{3,2,1,0:T(8,128)(2,1)S(1)} %slice_bitcast_fusion), channel_id=1, source_target_pairs={{0,32},{32,64},{64,96},{96,0},{1,33},{33,65},{65,97},{97,1},{2,34}... | collective-permute-start | bytes 393224 | tf_op jit(solution)/shard_map/ppermute | solution.py:19
  11.0 2.6 %fusion.46 = f32[512,512]{1,0:T(8,128)} fusion(bf16[512,512]{1,0:T(8,128)(2,1)} %param.17, bf16[3,512,512]{2,1,0:T(8,128)(2,1)} %param.32), kind=kOutput, calls=%fused_computation.70 | convolution fusion | flops 268435456 | bytes 2097152 | tf_op jit(solution)/shard_map/dot_general | solution.py:43
  16.5 5.7 %collective-permute-start.3 = (bf16[3,1,128,512]{3,2,1,0:T(8,128)(2,1)S(1)}, bf16[3,1,128,512]{3,2,1,0:T(8,128)(2,1)S(1)}, u32[]{:S(2)}, u32[]{:S(2)}) collective-permute-start(bf16[3,1,128,512]{3,2,1,0:T(8,128)(2,1)S(1)} %pad_maximum_fusion.1), channel_id=1, source_target_pairs={{1,0},{2,1},{3,2},{4,3},{5,4},{6,5},{7,6},{8,7},{9,8},{10,9},{11,1... | collective-permute-start | bytes 1179656 | tf_op jit(solution)/shard_map/ppermute | solution.py:20
  23.7 3.7 %collective-permute-done.2 = bf16[3,1,128,512]{3,2,1,0:T(8,128)(2,1)S(1)} collective-permute-done((bf16[3,1,128,512]{3,2,1,0:T(8,128)(2,1)S(1)}, bf16[3,1,128,512]{3,2,1,0:T(8,128)(2,1)S(1)}, u32[]{:S(2)}, u32[]{:S(2)}) %collective-permute-start.2) | collective-permute-done | bytes 393248 | tf_op jit(solution)/shard_map/ppermute | solution.py:19
  27.7 8.2 %fusion.5 = bf16[4096,512]{1,0:T(8,128)(2,1)S(1)} fusion(s32[4096]{0:T(1024)S(1)} %select_bitcast_fusion.1, bf16[1152,512]{1,0:T(8,128)(2,1)S(1)} %bitcast.141, bf16[512,512]{1,0:T(8,128)(2,1)S(1)} %copy-done), kind=kOutput, calls=%fused_computation.15 | convolution fusion | flops 6991642624 | bytes 5914624 | tf_op jit(solution)/shard_map/while/body/eval_jaxpr/dot_general | solution.py:76
  35.9 3.9 %multiply_convert_fusion.1 = bf16[32,128,512]{2,1,0:T(8,128)(2,1)S(1)} fusion(f32[128,512]{1,0:T(8,128)S(1)} %convolution_add_fusion.5, bf16[32,128,512]{2,1,0:T(8,128)(2,1)S(1)} %bitcast.157, bf16[3,512,512]{2,1,0:T(8,128)(2,1)S(1)} %copy-done.3), kind=kOutput, calls=%fused_computation.12 | convolution fusion | flops 2160066560 | bytes 9175040 | tf_op jit(solution)/shard_map/while/body/eval_jaxpr/dot_general | solution.py:43
  39.8 2.4 %fusion.115 = (f32[4096]{0:T(1024)S(1)}, f32[4096,512]{1,0:T(8,128)S(1)}) fusion(bf16[4096,512]{1,0:T(8,128)(2,1)S(1)} %bitcast.137, bf16[3,512,512]{2,1,0:T(8,128)(2,1)S(1)} %copy-done.3), kind=kOutput, calls=%fused_computation.210 | convolution fusion | flops 2149576704 | bytes 13123584 | tf_op jit(solution)/shard_map/while/body/eval_jaxpr/dot_general | solution.py:48
  46.0 1.7 %fusion.116 = (f32[128]{0:T(128)S(1)}, f32[128,512]{1,0:T(8,128)S(1)}) fusion(bf16[3,512,512]{2,1,0:T(8,128)(2,1)} %param.24, f32[128,512]{1,0:T(8,128)S(1)} %fusion.44, f32[512]{0:T(512)S(1)} %bitcast.154, bf16[128,512]{1,0:T(8,128)(2,1)S(1)} %select_reduce_fusion.1), kind=kOutput, calls=%fused_computation.211 | convolution fusion | flops 134741888 | bytes 1706496 | tf_op jit(solution)/shard_map/dot_general | solution.py:48
  48.5 3.0 %collective-permute-start.5 = (bf16[1,1,32,512]{3,2,1,0:T(8,128)(2,1)S(1)}, bf16[1,1,32,512]{3,2,1,0:T(8,128)(2,1)S(1)}, u32[]{:S(2)}, u32[]{:S(2)}) collective-permute-start(bf16[1,1,32,512]{3,2,1,0:T(8,128)(2,1)S(1)} %slice_bitcast_fusion.2), channel_id=1, source_target_pairs={{32,0},{64,32},{96,64},{0,96},{33,1},{65,33},{97,65},{1,97},{34,2}... | collective-permute-start | bytes 98312 | tf_op jit(solution)/shard_map/ppermute | solution.py:20
  52.2 5.5 %all-to-all-start = ((bf16[64,4,512]{2,1,0:T(4,128)(2,1)}), bf16[64,4,512]{2,1,0:T(4,128)(2,1)S(1)}, u32[]{:S(2)}, u32[]{:S(2)}) async-start(bf16[64,4,512]{2,1,0:T(4,128)(2,1)} %broadcast_in_dim.127), calls=%async_computation | async-start | bytes 524288 | tf_op jit(solution)/shard_map/all_to_all | solution.py:27
  57.7 2.0 %convolution_add_fusion.3 = f32[128,512]{1,0:T(8,128)} fusion(bf16[128,512]{1,0:T(8,128)(2,1)S(1)} %add_convert_fusion.2, bf16[3,512,512]{2,1,0:T(8,128)(2,1)} %param.26, f32[512]{0:T(512)S(1)} %bitcast.147), kind=kOutput, calls=%fused_computation.32 | convolution fusion | flops 67174400 | bytes 919552 | tf_op jit(solution)/shard_map/dot_general | solution.py:43
  59.7 1.9 %collective-permute-start.6 = (bf16[3,1,32,512]{3,2,1,0:T(8,128)(2,1)S(1)}, bf16[3,1,32,512]{3,2,1,0:T(8,128)(2,1)S(1)}, u32[]{:S(2)}, u32[]{:S(2)}) collective-permute-start(bf16[3,1,32,512]{3,2,1,0:T(8,128)(2,1)S(1)} %pad_maximum_fusion.4), channel_id=1, source_target_pairs={{0,1},{1,2},{2,3},{3,4},{4,5},{5,6},{6,7},{7,8},{8,9},{9,10},{10,1... | collective-permute-start | bytes 294920 | tf_op jit(solution)/shard_map/ppermute | solution.py:19
  61.6 4.1 %collective-permute-start.7 = (bf16[3,1,32,512]{3,2,1,0:T(8,128)(2,1)S(1)}, bf16[3,1,32,512]{3,2,1,0:T(8,128)(2,1)S(1)}, u32[]{:S(2)}, u32[]{:S(2)}) collective-permute-start(bf16[3,1,32,512]{3,2,1,0:T(8,128)(2,1)S(1)} %pad_maximum_fusion.4), channel_id=1, source_target_pairs={{1,0},{2,1},{3,2},{4,3},{5,4},{6,5},{7,6},{8,7},{9,8},{10,9},{11,1... | collective-permute-start | bytes 294920 | tf_op jit(solution)/shard_map/ppermute | solution.py:20
  67.0 2.4 %collective-permute-done.6 = bf16[3,1,32,512]{3,2,1,0:T(8,128)(2,1)S(1)} collective-permute-done((bf16[3,1,32,512]{3,2,1,0:T(8,128)(2,1)S(1)}, bf16[3,1,32,512]{3,2,1,0:T(8,128)(2,1)S(1)}, u32[]{:S(2)}, u32[]{:S(2)}) %collective-permute-start.6) | collective-permute-done | bytes 98336 | tf_op jit(solution)/shard_map/ppermute | solution.py:19
  69.5 4.2 %all_to_all.10 = bf16[2,64,4,512]{3,2,1,0:T(4,128)(2,1)S(1)} all-to-all(bf16[2,64,4,512]{3,2,1,0:T(4,128)(2,1)S(1)} %broadcast_in_dim.128), channel_id=1, replica_groups=mesh['gx'=4,'gy_0'=4,'gy_1'=4,'gy_2'=2] {'gy_2'}, dimensions={0} | all-to-all | bytes 1048576 | tf_op jit(solution)/shard_map/all_to_all | solution.py:27
  74.0 5.0 %fusion.4 = bf16[4096,512]{1,0:T(8,128)(2,1)S(1)} fusion(s32[4096]{0:T(1024)S(1)} %select_bitcast_fusion, bf16[512,512]{1,0:T(8,128)(2,1)S(1)} %reshape_reshape.3, bf16[288,512]{1,0:T(8,128)(2,1)S(1)} %bitcast.142, bf16[128,512]{1,0:T(8,128)(2,1)S(1)} %add_convert_fusion.2), kind=kOutput, calls=%fused_computation.14 | convolution fusion | flops 3901063168 | bytes 5160960 | tf_op jit(solution)/shard_map/while/body/eval_jaxpr/dot_general | solution.py:76
  79.0 3.8 %multiply_convert_fusion = bf16[32,128,512]{2,1,0:T(8,128)(2,1)S(1)} fusion(f32[128,512]{1,0:T(8,128)S(1)} %copy-done.6, bf16[32,128,512]{2,1,0:T(8,128)(2,1)S(1)} %bitcast.156, bf16[3,512,512]{2,1,0:T(8,128)(2,1)S(1)} %copy-done.4), kind=kOutput, calls=%fused_computation.8 | convolution fusion | flops 2160066560 | bytes 9175040 | tf_op jit(solution)/shard_map/while/body/eval_jaxpr/dot_general | solution.py:43
  82.8 2.4 %fusion.119 = (f32[4096]{0:T(1024)S(1)}, f32[4096,512]{1,0:T(8,128)S(1)}) fusion(bf16[4096,512]{1,0:T(8,128)(2,1)S(1)} %bitcast.138, bf16[3,512,512]{2,1,0:T(8,128)(2,1)S(1)} %copy-done.4), kind=kOutput, calls=%fused_computation.212 | convolution fusion | flops 2149576704 | bytes 13123584 | tf_op jit(solution)/shard_map/while/body/eval_jaxpr/dot_general | solution.py:48
  89.1 1.7 %fusion.120 = (f32[128]{0:T(128)S(1)}, f32[128,512]{1,0:T(8,128)S(1)}) fusion(bf16[3,512,512]{2,1,0:T(8,128)(2,1)} %param.28, f32[128,512]{1,0:T(8,128)S(1)} %fusion.35, f32[512]{0:T(512)S(1)} %bitcast.153, bf16[128,512]{1,0:T(8,128)(2,1)S(1)} %select_reduce_fusion), kind=kOutput, calls=%fused_computation.213 | convolution fusion | flops 134741888 | bytes 1706496 | tf_op jit(solution)/shard_map/dot_general | solution.py:48
  91.9 2.6 %collective-permute-start.9 = (bf16[1,1,32,512]{3,2,1,0:T(8,128)(2,1)S(1)}, bf16[1,1,32,512]{3,2,1,0:T(8,128)(2,1)S(1)}, u32[]{:S(2)}, u32[]{:S(2)}) collective-permute-start(bf16[1,1,32,512]{3,2,1,0:T(8,128)(2,1)S(1)} %slice_bitcast_fusion.1), channel_id=1, source_target_pairs={{32,0},{64,32},{96,64},{0,96},{33,1},{65,33},{97,65},{1,97},{34,2}... | collective-permute-start | bytes 98312 | tf_op jit(solution)/shard_map/ppermute | solution.py:20
  94.5 1.9 %collective-permute-done.8 = bf16[1,1,32,512]{3,2,1,0:T(8,128)(2,1)S(1)} collective-permute-done((bf16[1,1,32,512]{3,2,1,0:T(8,128)(2,1)S(1)}, bf16[1,1,32,512]{3,2,1,0:T(8,128)(2,1)S(1)}, u32[]{:S(2)}, u32[]{:S(2)}) %collective-permute-start.8) | collective-permute-done | bytes 32800 | tf_op jit(solution)/shard_map/ppermute | solution.py:19
  96.5 5.1 %collective-permute-start.11 = (bf16[3,1,32,512]{3,2,1,0:T(8,128)(2,1)S(1)}, bf16[3,1,32,512]{3,2,1,0:T(8,128)(2,1)S(1)}, u32[]{:S(2)}, u32[]{:S(2)}) collective-permute-start(bf16[3,1,32,512]{3,2,1,0:T(8,128)(2,1)S(1)} %pad_maximum_fusion.5), channel_id=1, source_target_pairs={{1,0},{2,1},{3,2},{4,3},{5,4},{6,5},{7,6},{8,7},{9,8},{10,9},{11,1... | collective-permute-start | bytes 294920 | tf_op jit(solution)/shard_map/ppermute | solution.py:20
  101.8 2.0 %collective-permute-done.10 = bf16[3,1,32,512]{3,2,1,0:T(8,128)(2,1)S(1)} collective-permute-done((bf16[3,1,32,512]{3,2,1,0:T(8,128)(2,1)S(1)}, bf16[3,1,32,512]{3,2,1,0:T(8,128)(2,1)S(1)}, u32[]{:S(2)}, u32[]{:S(2)}) %collective-permute-start.10) | collective-permute-done | bytes 98336 | tf_op jit(solution)/shard_map/ppermute | solution.py:19
  109.8 2.2 %fusion.124 = (f32[512]{0:T(512)S(1)}, f32[512,512]{0,1:T(8,128)S(1)}) fusion(bf16[3,512,512]{2,1,0:T(8,128)(2,1)} %param.32, f32[512,512]{1,0:T(8,128)S(1)} %copy-done.2, f32[512]{0:T(512)S(1)} %bitcast.155, bf16[512,512]{1,0:T(8,128)(2,1)S(1)} %select_reduce_fusion.2), kind=kOutput, calls=%fused_computation.215 | convolution fusion | flops 538967552 | bytes 3674112 | tf_op jit(solution)/shard_map/dot_general | solution.py:48
  (101 shorter events, 32.6 us)
Async XLA Ops:
  0.6 21.6 %copy-start = (bf16[512,512]{1,0:T(8,128)(2,1)S(1)}, bf16[512,512]{1,0:T(8,128)(2,1)}, u32[]{:S(2)}) copy-start(bf16[512,512]{1,0:T(8,128)(2,1)} %param.17) | copy-start | bytes 1572868
  0.6 14.4 %copy-start.1 = (bf16[128,512]{1,0:T(8,128)(2,1)S(1)}, bf16[128,512]{1,0:T(8,128)(2,1)}, u32[]{:S(2)}) copy-start(bf16[128,512]{1,0:T(8,128)(2,1)} %param.18) | copy-start | bytes 393220
  0.7 15.6 %copy-start.9 = (f32[2,512]{1,0:T(2,128)S(1)}, f32[2,512]{1,0:T(2,128)}, u32[]{:S(2)}) copy-start(f32[2,512]{1,0:T(2,128)} %param.29) | copy-start | bytes 12292
  0.7 21.5 %copy-start.10 = (f32[2,512]{1,0:T(2,128)S(1)}, f32[2,512]{1,0:T(2,128)}, u32[]{:S(2)}) copy-start(f32[2,512]{1,0:T(2,128)} %param.31) | copy-start | bytes 12292
  1.6 14.7 %collective-permute-start = (bf16[1,1,128,512]{3,2,1,0:T(8,128)(2,1)S(1)}, bf16[1,1,128,512]{3,2,1,0:T(8,128)(2,1)S(1)}, u32[]{:S(2)}, u32[]{:S(2)}) collective-permute-start(bf16[1,1,128,512]{3,2,1,0:T(8,128)(2,1)S(1)} %slice_bitcast_fusion), channel_id=1, source_target_pairs={{0,32},{32,64},{64,96},{96,0},{1,33},{33,65},{65,97},{97,1},{2,34}... | collective-permute-start | bytes 393224 | tf_op jit(solution)/shard_map/ppermute | solution.py:19
  3.3 13.0 %collective-permute-start.1 = (bf16[1,1,128,512]{3,2,1,0:T(8,128)(2,1)S(1)}, bf16[1,1,128,512]{3,2,1,0:T(8,128)(2,1)S(1)}, u32[]{:S(2)}, u32[]{:S(2)}) collective-permute-start(bf16[1,1,128,512]{3,2,1,0:T(8,128)(2,1)S(1)} %slice_bitcast_fusion), channel_id=1, source_target_pairs={{32,0},{64,32},{96,64},{0,96},{33,1},{65,33},{97,65},{1,97},{34,2}... | collective-permute-start | bytes 393224 | tf_op jit(solution)/shard_map/ppermute | solution.py:20
  16.4 11.0 %collective-permute-start.2 = (bf16[3,1,128,512]{3,2,1,0:T(8,128)(2,1)S(1)}, bf16[3,1,128,512]{3,2,1,0:T(8,128)(2,1)S(1)}, u32[]{:S(2)}, u32[]{:S(2)}) collective-permute-start(bf16[3,1,128,512]{3,2,1,0:T(8,128)(2,1)S(1)} %pad_maximum_fusion.1), channel_id=1, source_target_pairs={{0,1},{1,2},{2,3},{3,4},{4,5},{5,6},{6,7},{7,8},{8,9},{9,10},{10,1... | collective-permute-start | bytes 1179656 | tf_op jit(solution)/shard_map/ppermute | solution.py:19
  16.5 11.0 %collective-permute-start.3 = (bf16[3,1,128,512]{3,2,1,0:T(8,128)(2,1)S(1)}, bf16[3,1,128,512]{3,2,1,0:T(8,128)(2,1)S(1)}, u32[]{:S(2)}, u32[]{:S(2)}) collective-permute-start(bf16[3,1,128,512]{3,2,1,0:T(8,128)(2,1)S(1)} %pad_maximum_fusion.1), channel_id=1, source_target_pairs={{1,0},{2,1},{3,2},{4,3},{5,4},{6,5},{7,6},{8,7},{9,8},{10,9},{11,1... | collective-permute-start | bytes 1179656 | tf_op jit(solution)/shard_map/ppermute | solution.py:20
  27.6 8.3 %copy-start.3 = (bf16[3,512,512]{2,1,0:T(8,128)(2,1)S(1)}, bf16[3,512,512]{2,1,0:T(8,128)(2,1)}, u32[]{:S(2)}) copy-start(bf16[3,512,512]{2,1,0:T(8,128)(2,1)} %param.22) | copy-start | bytes 4718596
  48.1 11.6 %collective-permute-start.4 = (bf16[1,1,32,512]{3,2,1,0:T(8,128)(2,1)S(1)}, bf16[1,1,32,512]{3,2,1,0:T(8,128)(2,1)S(1)}, u32[]{:S(2)}, u32[]{:S(2)}) collective-permute-start(bf16[1,1,32,512]{3,2,1,0:T(8,128)(2,1)S(1)} %slice_bitcast_fusion.2), channel_id=1, source_target_pairs={{0,32},{32,64},{64,96},{96,0},{1,33},{33,65},{65,97},{97,1},{2,34}... | collective-permute-start | bytes 98312 | tf_op jit(solution)/shard_map/ppermute | solution.py:19
  48.5 11.2 %collective-permute-start.5 = (bf16[1,1,32,512]{3,2,1,0:T(8,128)(2,1)S(1)}, bf16[1,1,32,512]{3,2,1,0:T(8,128)(2,1)S(1)}, u32[]{:S(2)}, u32[]{:S(2)}) collective-permute-start(bf16[1,1,32,512]{3,2,1,0:T(8,128)(2,1)S(1)} %slice_bitcast_fusion.2), channel_id=1, source_target_pairs={{32,0},{64,32},{96,64},{0,96},{33,1},{65,33},{97,65},{1,97},{34,2}... | collective-permute-start | bytes 98312 | tf_op jit(solution)/shard_map/ppermute | solution.py:20
  52.2 17.2 %all-to-all-start = ((bf16[64,4,512]{2,1,0:T(4,128)(2,1)}), bf16[64,4,512]{2,1,0:T(4,128)(2,1)S(1)}, u32[]{:S(2)}, u32[]{:S(2)}) async-start(bf16[64,4,512]{2,1,0:T(4,128)(2,1)} %broadcast_in_dim.127), calls=%async_computation | async-start | bytes 524288 | tf_op jit(solution)/shard_map/all_to_all | solution.py:27
  59.7 9.6 %collective-permute-start.6 = (bf16[3,1,32,512]{3,2,1,0:T(8,128)(2,1)S(1)}, bf16[3,1,32,512]{3,2,1,0:T(8,128)(2,1)S(1)}, u32[]{:S(2)}, u32[]{:S(2)}) collective-permute-start(bf16[3,1,32,512]{3,2,1,0:T(8,128)(2,1)S(1)} %pad_maximum_fusion.4), channel_id=1, source_target_pairs={{0,1},{1,2},{2,3},{3,4},{4,5},{5,6},{6,7},{7,8},{8,9},{9,10},{10,1... | collective-permute-start | bytes 294920 | tf_op jit(solution)/shard_map/ppermute | solution.py:19
  61.6 7.7 %collective-permute-start.7 = (bf16[3,1,32,512]{3,2,1,0:T(8,128)(2,1)S(1)}, bf16[3,1,32,512]{3,2,1,0:T(8,128)(2,1)S(1)}, u32[]{:S(2)}, u32[]{:S(2)}) collective-permute-start(bf16[3,1,32,512]{3,2,1,0:T(8,128)(2,1)S(1)} %pad_maximum_fusion.4), channel_id=1, source_target_pairs={{1,0},{2,1},{3,2},{4,3},{5,4},{6,5},{7,6},{8,7},{9,8},{10,9},{11,1... | collective-permute-start | bytes 294920 | tf_op jit(solution)/shard_map/ppermute | solution.py:20
  74.0 5.0 %copy-start.4 = (bf16[3,512,512]{2,1,0:T(8,128)(2,1)S(1)}, bf16[3,512,512]{2,1,0:T(8,128)(2,1)}, u32[]{:S(2)}) copy-start(bf16[3,512,512]{2,1,0:T(8,128)(2,1)} %param.26) | copy-start | bytes 4718596
  74.0 5.0 %copy-start.6 = (f32[128,512]{1,0:T(8,128)S(1)}, f32[128,512]{1,0:T(8,128)}, u32[]{:S(2)}) copy-start(f32[128,512]{1,0:T(8,128)} %convolution_add_fusion.3) | copy-start | bytes 786436
  89.0 5.5 %copy-start.8 = (s32[3,512]{1,0:T(4,128)S(1)}, s32[3,512]{1,0:T(4,128)}, u32[]{:S(2)}) copy-start(s32[3,512]{1,0:T(4,128)} %param.21) | copy-start | bytes 18436
  89.1 12.5 %copy-start.11 = (f32[2,512]{1,0:T(2,128)S(1)}, f32[2,512]{1,0:T(2,128)}, u32[]{:S(2)}) copy-start(f32[2,512]{1,0:T(2,128)} %param.33) | copy-start | bytes 12292
  91.2 13.8 %copy-start.7 = (bf16[128,512]{1,0:T(8,128)(2,1)}, bf16[128,512]{1,0:T(8,128)(2,1)S(1)}, u32[]{:S(2)}) copy-start(bf16[128,512]{1,0:T(8,128)(2,1)S(1)} %add_convert_fusion.1) | copy-start | bytes 393220
  91.2 5.2 %collective-permute-start.8 = (bf16[1,1,32,512]{3,2,1,0:T(8,128)(2,1)S(1)}, bf16[1,1,32,512]{3,2,1,0:T(8,128)(2,1)S(1)}, u32[]{:S(2)}, u32[]{:S(2)}) collective-permute-start(bf16[1,1,32,512]{3,2,1,0:T(8,128)(2,1)S(1)} %slice_bitcast_fusion.1), channel_id=1, source_target_pairs={{0,32},{32,64},{64,96},{96,0},{1,33},{33,65},{65,97},{97,1},{2,34}... | collective-permute-start | bytes 98312 | tf_op jit(solution)/shard_map/ppermute | solution.py:19
  91.9 4.5 %collective-permute-start.9 = (bf16[1,1,32,512]{3,2,1,0:T(8,128)(2,1)S(1)}, bf16[1,1,32,512]{3,2,1,0:T(8,128)(2,1)S(1)}, u32[]{:S(2)}, u32[]{:S(2)}) collective-permute-start(bf16[1,1,32,512]{3,2,1,0:T(8,128)(2,1)S(1)} %slice_bitcast_fusion.1), channel_id=1, source_target_pairs={{32,0},{64,32},{96,64},{0,96},{33,1},{65,33},{97,65},{1,97},{34,2}... | collective-permute-start | bytes 98312 | tf_op jit(solution)/shard_map/ppermute | solution.py:20
  96.4 7.4 %collective-permute-start.10 = (bf16[3,1,32,512]{3,2,1,0:T(8,128)(2,1)S(1)}, bf16[3,1,32,512]{3,2,1,0:T(8,128)(2,1)S(1)}, u32[]{:S(2)}, u32[]{:S(2)}) collective-permute-start(bf16[3,1,32,512]{3,2,1,0:T(8,128)(2,1)S(1)} %pad_maximum_fusion.5), channel_id=1, source_target_pairs={{0,1},{1,2},{2,3},{3,4},{4,5},{5,6},{6,7},{7,8},{8,9},{9,10},{10,1... | collective-permute-start | bytes 294920 | tf_op jit(solution)/shard_map/ppermute | solution.py:19
  96.5 7.4 %collective-permute-start.11 = (bf16[3,1,32,512]{3,2,1,0:T(8,128)(2,1)S(1)}, bf16[3,1,32,512]{3,2,1,0:T(8,128)(2,1)S(1)}, u32[]{:S(2)}, u32[]{:S(2)}) collective-permute-start(bf16[3,1,32,512]{3,2,1,0:T(8,128)(2,1)S(1)} %pad_maximum_fusion.5), channel_id=1, source_target_pairs={{1,0},{2,1},{3,2},{4,3},{5,4},{6,5},{7,6},{8,7},{9,8},{10,9},{11,1... | collective-permute-start | bytes 294920 | tf_op jit(solution)/shard_map/ppermute | solution.py:20
  101.8 3.1 %copy-start.5 = (bf16[3,512,512]{2,1,0:T(8,128)(2,1)S(1)}, bf16[3,512,512]{2,1,0:T(8,128)(2,1)}, u32[]{:S(2)}) copy-start(bf16[3,512,512]{2,1,0:T(8,128)(2,1)} %param.30) | copy-start | bytes 4718596
  (1 other events, 1.2 us)
where the time goes:
time: 115 us; the launch traced here: 113 us
  matrix products  44.8 us (39%)
  starting transfers between devices  32.3 us (28%)
  other arithmetic  16.4 us (14%)
  waiting for transfers between devices  10.1 us (9%)
  local copies, waits for them, and re-layouts  4.44 us (4%)
  blocking collectives  4.15 us (4%)
  between operations  1.21 us (1%)
    ppermute x6, starting transfers between devices, with_halo(): after = lax.ppermute(initial, axis, down)  22.1 us
    dot_general x9, matrix products, project(): return jnp.dot(latent, weight, preferred_element_type=jnp.float32)  19 us
    dot_general x3, matrix products, one_block(): jnp.dot(selector, sources, preferred_element_type=jnp.float32)  14.2 us
    dot_general x6, matrix products, finish(): output = jnp.dot(hidden, weights[2], preferred_element_type=jnp.float32)  11.6 us
    ppermute x6, waiting for transfers between devices, with_halo(): before = lax.ppermute(last, axis, up)  9.97 us
    all_to_all x1, starting transfers between devices, from_everyone(): return lax.all_to_all(copies, axis, split_axis=0, concat_axis=0, tiled=True)  5.5 us
    ppermute x6, starting transfers between devices, with_halo(): before = lax.ppermute(last, axis, up)  4.75 us
    all_to_all x1, blocking collectives, from_everyone(): return lax.all_to_all(copies, axis, split_axis=0, concat_axis=0, tiled=True)  4.15 us
  transfers between devices with their start and end apart: 13, of which 5 were waited for; matrix products, arithmetic and copies ran while one was open for 15% of the time, Pallas kernels for 0%

commit v1 on v0

v1 whole, which is shorter than its diff:
```python
import functools

import jax
import jax.numpy as jnp
from jax import lax
from jax.experimental import pallas as pl
from jax.experimental.pallas import tpu as pltpu
from jax.sharding import PartitionSpec as P

MESH = pl.DeviceIdType.MESH
F32 = jnp.float32
BF16 = jnp.bfloat16

D = 512
G = 512
M = 128
K = 32
K3 = 3
CM = 4
GB = G // 4
MB = M // 4
NX = 4
NY = 32
CHIPS = NX * NY // 2

DEAD = 1
OWN = 2
RIM1 = OWN + G
ROWS1 = RIM1 + 9 * GB
RIM2 = OWN + M
COARSE = RIM2 + 9 * MB
ROWS2 = COARSE + 2 * CHIPS * CM
ROWS3 = COARSE

R = 16
BLOCKS = M // R
E = R * K
R3 = 128
BLOCKS3 = G // R3
E3 = R3 * K3


def log2(n):
    bits = n.bit_length() - 1
    assert n == 1 << bits
    return bits


def rows_of(ids, rows, border, rim, px, py):
    owner = lax.shift_right_arithmetic(ids, log2(rows))
    off = ids & (rows - 1)
    ox = lax.shift_right_arithmetic(owner, log2(NY))
    oy = owner & (NY - 1)
    dx = (ox - px) & (NX - 1)
    dy = (oy - py) & (NY - 1)
    sx = jnp.where(dx == 1, 2, jnp.where(dx == NX - 1, 0, 1))
    sy = jnp.where(dy == 1, 2, jnp.where(dy == NY - 1, 0, 1))
    near = ((dx <= 1) | (dx == NX - 1)) & ((dy <= 1) | (dy == NY - 1)) & (off < border)
    itself = (dx == 0) & (dy == 0)
    place = (owner & 1) * CHIPS + lax.shift_right_arithmetic(owner, 1)
    far = COARSE + place * CM + (off & (CM - 1))
    row = jnp.where(near, rim + (sx * 3 + sy) * border + off, far)
    row = jnp.where(itself, OWN + off, row)
    return jnp.where(ids < 0, DEAD, row)


def silu_half(y):
    return y * jnp.tanh(y) + y


def kernel(
    grid, mesh, encs, mshs, decs, w0, v0, w1, v1, w2, v2, w3, v3, w4, v4, w5, v5,
    out_grid, out_mesh,
    grid_v, mesh_v, encs_v, mshs_v, decs_v, w_v, v_v,
    pos1, pos2, pos3, idx_a, idx_b,
    tab1, tab2, tab3, base, nodebase, base3, nodebase3,
    gat_a, gat_b, hid_a, hid_b, mlp_a, mlp_b,
    aggb, enc_v, prc_v, dec_v, aggb3, hidn,
    send1, rim1, send2, rim2, coarse, send3, rim3,
    in_sem, w_sem, idx_sem, out_sem,
    s1_sem, r1_sem, s2_sem, r2_sem, s3_sem, r3_sem, sc_sem, rc_sem, sf_sem, rf_sem,
):
    px = lax.axis_index("gx")
    py = lax.axis_index("gy")
    core = py & 1
    chip = px * (NY // 2) + lax.shift_right_logical(py, 1)

    small = [
        (grid, grid_v), (mesh, mesh_v), (encs, encs_v), (mshs, mshs_v), (decs, decs_v),
        (v0, v_v.at[0]), (v1, v_v.at[1]), (v2, v_v.at[2]),
        (v3, v_v.at[3]), (v4, v_v.at[4]), (v5, v_v.at[5]),
    ]
    loads = [pltpu.make_async_copy(s, d, in_sem.at[i]) for i, (s, d) in enumerate(small)]
    wloads = [
        pltpu.make_async_copy(s, w_v.at[i], w_sem.at[i])
        for i, s in enumerate((w0, w1, w2, w3, w4, w5))
    ]
    loads[0].start()
    wloads[0].start()
    for c in loads[1:]:
        c.start()
    for i in (4, 5, 1, 2, 3):
        wloads[i].start()

    def at(dx, dy):
        return ((px + dx) & (NX - 1), (py + dy) & (NY - 1))

    def spread(buf, off, rows, value):
        for c in range(4):
            buf[pl.ds(off * 4 + c, rows, stride=4), :] = value[:, 128 * c : 128 * c + 128]

    def halo(src, rim, s_sem, r_sem, steps):
        copies = []
        for dx, dy in steps:
            slot = (1 - dx) * 3 + (1 - dy)
            copies.append(
                pltpu.make_async_remote_copy(
                    src_ref=src, dst_ref=rim.at[slot], send_sem=s_sem.at[slot],
                    recv_sem=r_sem.at[slot], device_id=at(dx, dy), device_id_type=MESH,
                )
            )
        for c in copies:
            c.start()
        return copies

    loads[0].wait()
    wloads[0].wait()
    own = jnp.dot(grid_v[0:GB, :], w_v[0, 0], preferred_element_type=F32) * 0.5
    spread(tab1, OWN, GB, own)
    send1[...] = tab1[OWN * 4 : (OWN + GB) * 4, :].astype(BF16)
    first = halo(send1, rim1, s1_sem, r1_sem, ((1, 0), (-1, 0), (0, 1), (0, -1)))

    for c in loads[1:]:
        c.wait()
    own = jnp.dot(grid_v[GB:G, :], w_v[0, 0], preferred_element_type=F32) * 0.5
    spread(tab1, OWN + GB, G - GB, own)
    dead = jnp.full((8, 128), -1e30, F32)
    for t in (tab1, tab2, tab3):
        t[0:8, :] = dead
    for t, rows in ((tab1, ROWS1), (tab2, ROWS2), (tab3, ROWS3)):
        t[rows * 4 : rows * 4 + 8, :] = dead

    lane = lax.broadcasted_iota(jnp.int32, (M, K), 0)
    odd = (lane & 1) * 4
    for src, pos, rows, border, rim in ((encs_v, pos1, G, GB, RIM1), (mshs_v, pos2, M, MB, RIM2)):
        row = rows_of(src[...], rows, border, rim, px, py)
        pos[0:M, :] = jnp.zeros((M, 128), jnp.int32)
        pos[M : M + 2 * R, :] = jnp.zeros((2 * R, 128), jnp.int32)
        pos[0:M, 0:K] = row.T * 4 - odd
    odd3 = (lax.broadcasted_iota(jnp.int32, (K3, R3), 1) & 1) * 4
    pos3[...] = jnp.zeros(pos3.shape, jnp.int32)
    for b in range(BLOCKS3):
        row = rows_of(decs_v[:, R3 * b : R3 * b + R3], M, MB, RIM2, px, py)
        pos3[b, 0:K3, :] = row * 4 - odd3

    def centre(i):
        def some(j, carry):
            at_rows = pl.ds(pl.multiple_of(j * 64, 64), 64)
            w = w_v[i, 2, at_rows, :].astype(F32)
            w_v[i, 2, at_rows, :] = (w - jnp.mean(w, axis=1, keepdims=True)).astype(BF16)
            return carry

        lax.fori_loop(0, D // 64, some, 0)

    def bias(i):
        return v_v[i, 0:1, :]

    def gain(i):
        return 1.0 + v_v[i, 1:2, :]

    def dot(a, b):
        return jnp.dot(a, b, preferred_element_type=F32)

    base[...] = (dot(mesh_v[...], w_v[0, 1]) + bias(0)) * 0.5
    centre(0)
    for i in (4, 5, 1, 2, 3):
        wloads[i].wait()
        centre(i)
    nodebase[...] = dot(mesh_v[...], w_v[1, 0]) + bias(1)
    base3[...] = (dot(grid_v[...], w_v[4, 1]) + bias(4)) * 0.5
    nodebase3[...] = dot(grid_v[...], w_v[5, 0]) + bias(5)

    first[0].wait_recv()
    first[1].wait_recv()
    second = []
    for sx in (0, 2):
        for dy in (1, -1):
            slot = sx * 3 + 1 - dy
            second.append(
                pltpu.make_async_remote_copy(
                    src_ref=rim1.at[sx * 3 + 1], dst_ref=rim1.at[slot], send_sem=s1_sem.at[slot],
                    recv_sem=r1_sem.at[slot], device_id=at(0, dy), device_id_type=MESH,
                )
            )
    for c in second:
        c.start()
    for c in first[2:] + second:
        c.wait_recv()
    for slot in (0, 1, 2, 3, 5, 6, 7, 8):
        lo = (RIM1 + slot * GB) * 4
        tab1[lo : lo + GB * 4, :] = rim1[slot].astype(F32)
    for c in first + second:
        c.wait_send()

    def update(i, rows, x, agg, node, new):
        n = rows.size
        p = node[rows, :] + dot(agg[rows, :], w_v[i, 1])
        o = dot(silu_half(p * 0.5).astype(BF16), w_v[i, 2])
        s = lax.rsqrt(jnp.mean(o * o, axis=1, keepdims=True) + 1e-5)
        new[rows, :] = (x[rows, :].astype(F32) + o * s * gain(i)).astype(BF16)

    def gather(tab, idx, gat, slots, receivers, by_row):
        low = lax.broadcasted_iota(jnp.int32, (8, 128), 0) < 4
        for k in range(slots):
            for r in range(0, receivers, 2):
                ia = idx[r, k] if by_row else idx[k, r]
                ib = idx[r + 1, k] if by_row else idx[k, r + 1]
                e = k * receivers + r
                gat[4 * e : 4 * e + 8, :] = jnp.where(low, tab[pl.ds(ia, 8), :], tab[pl.ds(ib, 8), :])

    def messages(i, gat, hid, mlp, slots, receivers, base_ref, base_row, agg):
        for c in range(4):
            cols = slice(128 * c, 128 * c + 128)
            for r in range(0, receivers, 16):
                b = base_ref[pl.ds(base_row + r, 16), cols]
                for k in range(slots):
                    e = k * receivers + r
                    y = gat[pl.ds(4 * e + c, 16, stride=4), :] + b
                    hid[e : e + 16, cols] = silu_half(y).astype(BF16)
        edges = slots * receivers
        mlp[0:edges, :] = dot(hid[0:edges, :], w_v[i, 2])
        g = gain(i)
        for r in range(0, receivers, 16):
            total = jnp.zeros((16, D), F32)
            for k in range(slots):
                e = k * receivers + r
                o = mlp[e : e + 16, :]
                total += o * lax.rsqrt(jnp.mean(o * o, axis=1, keepdims=True) + 1e-5)
            agg[pl.ds(base_row + r, 16), :] = (total * g).astype(BF16)

    def mesh_step(i, tab, pos, after_first):
        def fetch(b, idx, sem):
            return pltpu.make_async_copy(pos.at[pl.ds(pl.multiple_of(b * R, R), R), :], idx, sem)

        fetch(0, idx_a, idx_sem.at[0]).start()
        fetch(1, idx_b, idx_sem.at[1]).start()
        fetch(0, idx_a, idx_sem.at[0]).wait()
        gather(tab, idx_a, gat_a, K, R, True)

        def two(j, carry):
            fetch(2 * j + 2, idx_a, idx_sem.at[0]).start()
            fetch(2 * j + 1, idx_b, idx_sem.at[1]).wait()
            gather(tab, idx_b, gat_b, K, R, True)
            row = pl.multiple_of(j * (2 * R), 2 * R)
            messages(i, gat_a, hid_a, mlp_a, K, R, base, row, aggb)
            fetch(2 * j + 2, idx_a, idx_sem.at[0]).wait()
            fetch(2 * j + 3, idx_b, idx_sem.at[1]).start()
            gather(tab, idx_a, gat_a, K, R, True)
            messages(i, gat_b, hid_b, mlp_b, K, R, base, row + R, aggb)
            pl.when(j == 0)(after_first)
            return carry

        lax.fori_loop(0, BLOCKS // 2, two, 0)
        fetch(1, idx_b, idx_sem.at[1]).wait()

    ring = ((1, 0), (-1, 0), (0, 1), (0, -1), (1, 1), (1, -1), (-1, 1), (-1, -1))
    head = pl.ds(0, MB)
    tail = pl.ds(MB, M - MB)

    def halo_copies(src, rim, s_sem, r_sem):
        return [
            pltpu.make_async_remote_copy(
                src_ref=src, dst_ref=rim.at[(1 - dx) * 3 + 1 - dy],
                send_sem=s_sem.at[(1 - dx) * 3 + 1 - dy], recv_sem=r_sem.at[(1 - dx) * 3 + 1 - dy],
                device_id=at(dx, dy), device_id_type=MESH,
            )
            for dx, dy in ring
        ]

    coarse[core, chip] = jnp.zeros((4 * CM, 128), BF16)

    def coarse_copy(j):
        to = (chip + j) & (CHIPS - 1)
        return pltpu.make_async_remote_copy(
            src_ref=send2.at[0 : 4 * CM], dst_ref=coarse.at[core, chip], send_sem=sc_sem, recv_sem=rc_sem,
            device_id=(lax.shift_right_logical(to, log2(NY // 2)), (to & (NY // 2 - 1)) * 2 + core),
            device_id_type=MESH,
        )

    def coarse_all():
        return pltpu.make_async_remote_copy(
            src_ref=coarse.at[core, 0 : CHIPS - 1], dst_ref=coarse.at[core, 0 : CHIPS - 1],
            send_sem=sc_sem, recv_sem=rc_sem, device_id=at(0, 1), device_id_type=MESH,
        )

    def send_encoded():
        update(1, head, mesh_v, aggb, nodebase, enc_v)
        spread(tab2, OWN, MB, dot(enc_v[head, :], w_v[2, 0]) * 0.5)
        send2[...] = tab2[OWN * 4 : (OWN + MB) * 4, :].astype(BF16)

        def one(j, carry):
            coarse_copy(j).start()
            return carry

        lax.fori_loop(1, CHIPS, one, 0)
        for c in halo_copies(send2, rim2, s2_sem, r2_sem):
            c.start()

    mesh_step(0, tab1, pos1, send_encoded)
    update(1, tail, mesh_v, aggb, nodebase, enc_v)

    coarse_all().wait_recv()
    forward = pltpu.make_async_remote_copy(
        src_ref=coarse.at[core], dst_ref=coarse.at[core], send_sem=sf_sem, recv_sem=rf_sem,
        device_id=(px, py ^ 1), device_id_type=MESH,
    )
    forward.start()
    spread(tab2, OWN, M, dot(enc_v[...], w_v[2, 0]) * 0.5)
    base[...] = (dot(enc_v[...], w_v[2, 1]) + bias(2)) * 0.5
    nodebase[...] = dot(enc_v[...], w_v[3, 0]) + bias(3)
    copies = halo_copies(send2, rim2, s2_sem, r2_sem)
    for c in copies:
        c.wait_recv()
    for slot in (0, 1, 2, 3, 5, 6, 7, 8):
        lo = (RIM2 + slot * MB) * 4
        tab2[lo : lo + MB * 4, :] = rim2[slot].astype(F32)
    forward.wait_recv()
    for a in range(2):
        lo = (COARSE + a * CHIPS * CM) * 4
        tab2[lo : lo + CHIPS * CM * 4, :] = coarse[a].reshape(CHIPS * CM * 4, 128).astype(F32)
    for c in copies:
        c.wait_send()
    coarse_all().wait_send()
    forward.wait_send()

    def send_processed():
        update(3, head, enc_v, aggb, nodebase, prc_v)
        spread(tab3, OWN, MB, dot(prc_v[head, :], w_v[4, 0]) * 0.5)
        send3[...] = tab3[OWN * 4 : (OWN + MB) * 4, :].astype(BF16)
        for c in halo_copies(send3, rim3, s3_sem, r3_sem):
            c.start()

    mesh_step(2, tab2, pos2, send_processed)
    update(3, tail, enc_v, aggb, nodebase, prc_v)
    put_mesh = pltpu.make_async_copy(prc_v, out_mesh, out_sem.at[0])
    put_mesh.start()

    spread(tab3, OWN, M, dot(prc_v[...], w_v[4, 0]) * 0.5)
    copies = halo_copies(send3, rim3, s3_sem, r3_sem)
    for c in copies:
        c.wait_recv()
    for slot in (0, 1, 2, 3, 5, 6, 7, 8):
        lo = (RIM2 + slot * MB) * 4
        tab3[lo : lo + MB * 4, :] = rim3[slot].astype(F32)
    for c in copies:
        c.wait_send()

    def fetch3(b):
        return pltpu.make_async_copy(pos3.at[b], idx_a.at[0:8, :], idx_sem.at[0])

    def one3(b, carry):
        fetch3(b).start()
        fetch3(b).wait()
        gather(tab3, idx_a, gat_a, K3, R3, False)
        messages(4, gat_a, hid_a, mlp_a, K3, R3, base3, pl.multiple_of(b * R3, R3), aggb3)
        return carry

    lax.fori_loop(0, BLOCKS3, one3, 0)
    update(5, pl.ds(0, G), grid_v, aggb3, nodebase3, dec_v)
    put_grid = pltpu.make_async_copy(dec_v, out_grid, out_sem.at[1])
    put_grid.start()
    put_mesh.wait()
    put_grid.wait()


def per_device(*args):
    any_space = pl.BlockSpec(memory_space=pl.ANY)
    dma = pltpu.SemaphoreType.DMA
    vm = pltpu.VMEM
    i32 = jnp.int32
    return pl.pallas_call(
        kernel,
        out_shape=(jax.ShapeDtypeStruct((G, D), BF16), jax.ShapeDtypeStruct((M, D), BF16)),
        in_specs=[any_space] * len(args),
        out_specs=(any_space, any_space),
        scratch_shapes=[
            vm((G, D), BF16), vm((M, D), BF16), vm((K, M), i32), vm((K, M), i32), vm((K3, G), i32),
            vm((6, 3, D, D), BF16), vm((6, 2, D), F32),
            vm((M + 2 * R, 128), i32), vm((M + 2 * R, 128), i32), vm((BLOCKS3, 8, 128), i32),
            pltpu.SMEM((R, 128), i32), pltpu.SMEM((R, 128), i32),
            vm((ROWS1 * 4 + 8, 128), F32), vm((ROWS2 * 4 + 8, 128), F32), vm((ROWS3 * 4 + 8, 128), F32),
            vm((M, D), F32), vm((M, D), F32), vm((G, D), F32), vm((G, D), F32),
            vm((E * 4, 128), F32), vm((E * 4, 128), F32),
            vm((E, D), BF16), vm((E, D), BF16), vm((E, D), F32), vm((E, D), F32),
            vm((M, D), BF16), vm((M, D), BF16), vm((M, D), BF16), vm((G, D), BF16), vm((G, D), BF16), vm((M, D), BF16),
            vm((GB * 4, 128), BF16), vm((9, GB * 4, 128), BF16),
            vm((MB * 4, 128), BF16), vm((9, MB * 4, 128), BF16),
            vm((2, CHIPS, CM * 4, 128), BF16),
            vm((MB * 4, 128), BF16), vm((9, MB * 4, 128), BF16),
            dma((11,)), dma((6,)), dma((2,)), dma((2,)),
            dma((9,)), dma((9,)), dma((9,)), dma((9,)), dma((9,)), dma((9,)),
            dma, dma, dma, dma,
        ],
        compiler_params=pltpu.CompilerParams(has_side_effects=True, vmem_limit_bytes=60 * 1024 * 1024),
    )(*args)


def solution(mesh):
    assert dict(mesh.shape) == {"gx": NX, "gy": NY}
    split = P(("gx", "gy"), None)
    lists = P(None, ("gx", "gy"))
    return jax.shard_map(
        per_device,
        mesh=mesh,
        in_specs=(split, split, lists, lists, lists) + (P(),) * 12,
        out_specs=(split, split),
        check_vma=False,
    )
```

time: 115 us -> 62.4 us (0.54)
  Pallas kernels: 0 us -> 57.4 us
  matrix products: 44.8 us -> 0 us
  starting transfers between devices: 32.3 us -> 0 us
  other arithmetic: 16.4 us -> 0 us
  waiting for transfers between devices: 10.1 us -> 0 us
  blocking collectives: 4.15 us -> 0 us
    pallas_call x0 -> x1, Pallas kernels: none -> 57.4 us  [per_device(): pl.pallas_call(kernel, out_shape=(jax.ShapeDtypeStruct((G, D), BF16), jax...]
    dot_general x18 -> x0, matrix products: 44.8 us -> none  [the longest x9 19 us: project(): return jnp.dot(latent, weight, preferred_element_type=jnp.float32)]
    ppermute x12 -> x0, starting transfers between devices: 26.8 us -> none  [the longest x6 22.1 us: with_halo(): after = lax.ppermute(initial, axis, down)]
    ppermute x12 -> x0, waiting for transfers between devices: 10.1 us -> none  [the longest x6 9.97 us: with_halo(): before = lax.ppermute(last, axis, up)]
    reduce_sum x9 -> x0, other arithmetic: 6.04 us -> none  [the longest x6 4 us: finish(): spread = jnp.mean(centred * centred, axis=-1, keepdims=True)]
    all_to_all x1 -> x0, starting transfers between devices: 5.5 us -> none  [from_everyone(): return lax.all_to_all(copies, axis, split_axis=0, concat_axis=0, tiled=True)]
    all_to_all x1 -> x0, blocking collectives: 4.15 us -> none  [from_everyone(): return lax.all_to_all(copies, axis, split_axis=0, concat_axis=0, tiled=True)]
    mul x3 -> x0, other arithmetic: 3.39 us -> none  [finish(): return centred * lax.rsqrt(spread + 1e-05) * (1.0 + vectors[1])]
  transfers between devices with their start and end apart: 13 -> 0, of which waited for: 5 -> 0; matrix products, arithmetic and copies ran while one was open for 15% -> 0% of each run, Pallas kernels for 0% -> 0%
where the time goes in v1:
time: 62.4 us; the launch traced here: 61.5 us
  Pallas kernels  57.4 us (92%)
  local copies, waits for them, and re-layouts  3.44 us (6%)
  between operations  0.65 us (1%)
    pallas_call x1, Pallas kernels, per_device(): pl.pallas_call(kernel, out_shape=(jax.ShapeDtypeStruct((G, D), BF16), jax...  57.4 us
    unnamed x2, local copies, waits for them, and re-layouts  3.44 us

profile of v1, /device:TPU:0, one launch (start us, length us, event | category | flops | bytes accessed | tf_op | source)
XLA Modules:
  0.0 61.5 jit_solution(805395455193410916)
XLA Ops:
  0.6 57.4 %shard_map.176 = (bf16[512,512]{1,0:T(8,128)(2,1)}, bf16[128,512]{1,0:T(8,128)(2,1)}) custom-call(bf16[512,512]{1,0:T(8,128)(2,1)} %grid.1, bf16[128,512]{1,0:T(8,128)(2,1)} %mesh.1, s32[32,128]{1,0:T(8,128)} %encs.1, s32[32,128]{1,0:T(8,128)} %mshs.1, s32[3,512]{1,0:T(4,128)} %decs.1, bf16[3,512,512]{2,1,0:T(8,128)(2,1)} %w0.1, f32[2,512]{1,0:T(2,128)} %v0.1, ...), custom_call_target="tpu_custom_call" | custom-call | tf_op jit(solution)/shard_map/pallas_call | solution.py:381
  58.1 1.9 %copy.21 = bf16[512,512]{1,0:T(8,128)(2,1)} copy(bf16[512,512]{1,0:T(8,128)(2,1)} %get-tuple-element.4) | data formatting | bytes 1048576
  59.9 1.6 %copy.22 = bf16[128,512]{1,0:T(8,128)(2,1)} copy(bf16[128,512]{1,0:T(8,128)(2,1)} %get-tuple-element.5) | data formatting | bytes 262144

commit v2 on v1

v2 whole, which is shorter than its diff:
```python
import functools

import jax
import jax.numpy as jnp
from jax import lax
from jax.experimental import pallas as pl
from jax.experimental.pallas import tpu as pltpu
from jax.sharding import PartitionSpec as P

MESH = pl.DeviceIdType.MESH
F32 = jnp.float32
BF16 = jnp.bfloat16

D = 512
G = 512
M = 128
K = 32
K3 = 3
CM = 4
GB = G // 4
MB = M // 4
NX = 4
NY = 32
CHIPS = NX * NY // 2

DEAD = 1
OWN = 2
RIM1 = OWN + G
ROWS1 = RIM1 + 9 * GB
RIM2 = OWN + M
COARSE = RIM2 + 9 * MB
ROWS2 = COARSE + 2 * CHIPS * CM
ROWS3 = COARSE

R = 16
BLOCKS = M // R
E = R * K
R3 = 128
BLOCKS3 = G // R3
E3 = R3 * K3
HALF = GB * 2


def log2(n):
    bits = n.bit_length() - 1
    assert n == 1 << bits
    return bits


def rows_of(ids, rows, border, rim, px, py):
    owner = lax.shift_right_arithmetic(ids, log2(rows))
    off = ids & (rows - 1)
    ox = lax.shift_right_arithmetic(owner, log2(NY))
    oy = owner & (NY - 1)
    dx = (ox - px) & (NX - 1)
    dy = (oy - py) & (NY - 1)
    sx = jnp.where(dx == 1, 2, jnp.where(dx == NX - 1, 0, 1))
    sy = jnp.where(dy == 1, 2, jnp.where(dy == NY - 1, 0, 1))
    near = ((dx <= 1) | (dx == NX - 1)) & ((dy <= 1) | (dy == NY - 1)) & (off < border)
    itself = (dx == 0) & (dy == 0)
    place = (owner & 1) * CHIPS + lax.shift_right_arithmetic(owner, 1)
    far = COARSE + place * CM + (off & (CM - 1))
    row = jnp.where(near, rim + (sx * 3 + sy) * border + off, far)
    row = jnp.where(itself, OWN + off, row)
    return jnp.where(ids < 0, DEAD, row)


def silu_half(y):
    return y * jnp.tanh(y) + y


def kernel(
    grid, mesh, encs, mshs, decs, w0, v0, w1, v1, w2, v2, w3, v3, w4, v4, w5, v5,
    out_grid, out_mesh,
    grid_v, mesh_v, encs_v, mshs_v, decs_v, w_v, v_v,
    pos1, pos2, pos3, idx1, idx2, idx3,
    tab1, tab2, tab3, base, nodebase, base3, nodebase3,
    gat_a, gat_b, hid_a, hid_b, mlp_a, mlp_b,
    aggb, enc_v, prc_v, dec_v, aggb3,
    send1, rim1, send2, rim2, coarse, send3, rim3,
    in_sem, w_sem, idx_sem, out_sem,
    s1_sem, r1_sem, s2_sem, r2_sem, s3_sem, r3_sem, sc_sem, rc_sem, sf_sem, rf_sem,
    meet_a, meet_b,
):
    px = lax.axis_index("gx")
    py = lax.axis_index("gy")
    core = py & 1
    chip = px * (NY // 2) + lax.shift_right_logical(py, 1)

    def at(dx, dy):
        return ((px + dx) & (NX - 1), (py + dy) & (NY - 1))

    ring = ((1, 0), (-1, 0), (0, 1), (0, -1), (1, 1), (1, -1), (-1, 1), (-1, -1))
    z = lax.shift_right_logical(py, 1) & 3
    y = lax.shift_right_logical(py, 3)
    lines = [at(dx, 0) for dx in (1, 2, 3)]
    lines += [(px, (((y + d) & 3) * 4 + z) * 2 + core) for d in (1, 2, 3)]
    lines += [(px, (y * 4 + ((z + d) & 3)) * 2 + core) for d in (1, 2, 3)]
    partners = [at(*d) for d in ring] + [lines[1]] + lines[3:]

    border_load = pltpu.make_async_copy(grid.at[0:GB], grid_v.at[0:GB], in_sem.at[0])
    first_weight = pltpu.make_async_copy(w0.at[0], w_v.at[0, 0], w_sem.at[0])
    small = [
        (grid.at[GB:G], grid_v.at[GB:G]), (mesh, mesh_v), (encs, encs_v), (mshs, mshs_v), (decs, decs_v),
        (v0, v_v.at[0]), (v1, v_v.at[1]), (v2, v_v.at[2]),
        (v3, v_v.at[3]), (v4, v_v.at[4]), (v5, v_v.at[5]),
    ]
    loads = [pltpu.make_async_copy(s, d, in_sem.at[i + 1]) for i, (s, d) in enumerate(small)]
    wloads = {0: pltpu.make_async_copy(w0.at[1:3], w_v.at[0, 1:3], w_sem.at[6])}
    for i, s in enumerate((w1, w2, w3, w4, w5)):
        wloads[i + 1] = pltpu.make_async_copy(s, w_v.at[i + 1], w_sem.at[i + 1])
    border_load.start()
    first_weight.start()
    barrier = pltpu.get_barrier_semaphore()
    for p in partners:
        pl.semaphore_signal(barrier, inc=1, device_id=p, device_id_type=MESH)
    for c in loads:
        c.start()
    wloads[0].start()

    def spread(buf, off, rows, value):
        for c in range(4):
            buf[pl.ds(off * 4 + c, rows, stride=4), :] = value[:, 128 * c : 128 * c + 128]

    def dot(a, b):
        return jnp.dot(a, b, preferred_element_type=F32)

    def bias(i):
        return v_v[i, 0:1, :]

    def gain(i):
        return 1.0 + v_v[i, 1:2, :]

    def centre(i):
        def some(j, carry):
            at_rows = pl.ds(pl.multiple_of(j * 128, 128), 128)
            w = w_v[i, 2, at_rows, :].astype(F32)
            w_v[i, 2, at_rows, :] = (w - jnp.mean(w, axis=1, keepdims=True)).astype(BF16)
            return carry

        lax.fori_loop(0, D // 128, some, 0)

    def border_copy(src, sx, sy, to, half):
        slot = sx * 3 + sy
        return pltpu.make_async_remote_copy(
            src_ref=src, dst_ref=rim1.at[slot, half * HALF : half * HALF + HALF],
            send_sem=s1_sem.at[slot, half], recv_sem=r1_sem.at[slot, half],
            device_id=to, device_id_type=MESH,
        )

    border_load.wait()
    first_weight.wait()
    spread(tab1, OWN, GB, dot(grid_v[0:GB, :], w_v[0, 0]) * 0.5)
    send1[...] = tab1[OWN * 4 : (OWN + GB) * 4, :].astype(BF16)
    pl.semaphore_wait(barrier, len(partners))
    along_x = [[], []]
    along_y = [[], []]
    for half in range(2):
        part = send1.at[half * HALF : half * HALF + HALF]
        for d in (1, -1):
            along_x[half].append(border_copy(part, 1 - d, 1, at(d, 0), half))
            along_y[half].append(border_copy(part, 1, 1 - d, at(0, d), half))
    for half in range(2):
        for c in along_x[half] + along_y[half]:
            c.start()
    for i in (1, 4, 5, 2, 3):
        wloads[i].start()
    for p in lines:
        pl.semaphore_signal(meet_a, inc=1, device_id=p, device_id_type=MESH)

    for c in loads:
        c.wait()
    spread(tab1, OWN + GB, G - GB, dot(grid_v[GB:G, :], w_v[0, 0]) * 0.5)
    dead = jnp.full((8, 128), -1e30, F32)
    for t in (tab1, tab2, tab3):
        t[0:8, :] = dead
    for t, rows in ((tab1, ROWS1), (tab2, ROWS2), (tab3, ROWS3)):
        t[rows * 4 : rows * 4 + 8, :] = dead

    odd = (lax.broadcasted_iota(jnp.int32, (M, K), 0) & 1) * 4
    odd3 = (lax.broadcasted_iota(jnp.int32, (K3, R3), 1) & 1) * 4

    def place(src, pos, rows, border, rim):
        pos[...] = jnp.zeros(pos.shape, jnp.int32)
        pos[:, 0:K] = rows_of(src[...], rows, border, rim, px, py).T * 4 - odd

    place(encs_v, pos1, G, GB, RIM1)
    idx_loads = [
        pltpu.make_async_copy(pos, idx, idx_sem.at[i])
        for i, (pos, idx) in enumerate(((pos1, idx1), (pos2, idx2), (pos3, idx3)))
    ]
    idx_loads[0].start()
    wloads[0].wait()
    base[...] = (dot(mesh_v[...], w_v[0, 1]) + bias(0)) * 0.5
    pl.semaphore_wait(meet_a, len(lines))
    for p in lines:
        pl.semaphore_signal(meet_b, inc=1, device_id=p, device_id_type=MESH)

    corners = [[], []]
    for half in range(2):
        for sx in (0, 2):
            part = rim1.at[sx * 3 + 1, half * HALF : half * HALF + HALF]
            for d in (1, -1):
                corners[half].append(border_copy(part, sx, 1 - d, at(0, d), half))

    for c in along_x[0]:
        c.wait_recv()
    for c in corners[0]:
        c.start()
    centre(0)
    wloads[1].wait()
    centre(1)
    nodebase[...] = dot(mesh_v[...], w_v[1, 0]) + bias(1)
    for c in along_x[1]:
        c.wait_recv()
    for c in corners[1]:
        c.start()
    place(mshs_v, pos2, M, MB, RIM2)
    pos3[...] = jnp.zeros(pos3.shape, jnp.int32)
    for b in range(BLOCKS3):
        row = rows_of(decs_v[:, R3 * b : R3 * b + R3], M, MB, RIM2, px, py)
        pos3[8 * b : 8 * b + K3, :] = row * 4 - odd3
    idx_loads[1].start()
    idx_loads[2].start()
    for i in (4, 5, 2, 3):
        wloads[i].wait()
        centre(i)
    base3[...] = (dot(grid_v[...], w_v[4, 1]) + bias(4)) * 0.5
    nodebase3[...] = dot(grid_v[...], w_v[5, 0]) + bias(5)
    coarse[core, chip] = jnp.zeros((4 * CM, 128), BF16)

    def unpack(tab, first_row, rim, slots, rows):
        for slot in slots:
            lo = (first_row + slot * rows) * 4
            tab[lo : lo + rows * 4, :] = rim[slot].astype(F32)

    unpack(tab1, RIM1, rim1, (1, 7), GB)
    for c in along_y[0] + along_y[1]:
        c.wait_recv()
    unpack(tab1, RIM1, rim1, (3, 5), GB)
    for c in corners[0] + corners[1]:
        c.wait_recv()
    unpack(tab1, RIM1, rim1, (0, 2, 6, 8), GB)
    for half in range(2):
        for c in along_x[half] + along_y[half] + corners[half]:
            c.wait_send()
    for c in idx_loads:
        c.wait()
    pl.semaphore_wait(meet_b, len(lines))

    def update(i, rows, x, agg, node, new):
        kept = {}

        def one():
            kept["p"] = node[rows, :] + dot(agg[rows, :], w_v[i, 1])

        def two():
            kept["h"] = silu_half(kept["p"] * 0.5).astype(BF16)

        def three():
            kept["o"] = dot(kept["h"], w_v[i, 2])

        def four():
            o = kept["o"]
            s = lax.rsqrt(jnp.mean(o * o, axis=1, keepdims=True) + 1e-5)
            new[rows, :] = (x[rows, :].astype(F32) + o * s * gain(i)).astype(BF16)

        return [one, two, three, four]

    low = lax.broadcasted_iota(jnp.int32, (8, 128), 0) < 4

    def gather(tab, idx, gat, slots, receivers, where):
        def some(first, k):
            for r in range(0, 16, 2):
                ia, ib = idx[where(first + r, k)], idx[where(first + r + 1, k)]
                e = first * slots + k * 16 + r
                gat[4 * e : 4 * e + 8, :] = jnp.where(low, tab[pl.ds(ia, 8), :], tab[pl.ds(ib, 8), :])

        return [functools.partial(some, first, k) for first in range(0, receivers, 16) for k in range(slots)]

    def messages(i, gat, hid, mlp, slots, receivers, base_ref, base_row, agg, side):
        edges = slots * receivers
        places = [(first, k) for first in range(0, receivers, 16) for k in range(slots)]
        half = len(places) // 2

        def hidden(first, k):
            e = first * slots + k * 16
            for c in range(4):
                cols = slice(128 * c, 128 * c + 128)
                y = gat[pl.ds(4 * e + c, 16, stride=4), :] + base_ref[base_row + first : base_row + first + 16, cols]
                hid[e : e + 16, cols] = silu_half(y).astype(BF16)

        def product(lo, hi):
            mlp[lo:hi, :] = dot(hid[lo:hi, :], w_v[i, 2])

        kept = {}

        def collect(first, k):
            e = first * slots + k * 16
            o = mlp[e : e + 16, :]
            o = o * lax.rsqrt(jnp.mean(o * o, axis=1, keepdims=True) + 1e-5)
            kept["sum"] = o if k == 0 else kept["sum"] + o
            if k == slots - 1:
                agg[base_row + first : base_row + first + 16, :] = (kept["sum"] * gain(i)).astype(BF16)

        steps = [functools.partial(hidden, *p) for p in places[:half]]
        steps.append(functools.partial(product, 0, edges // 2))
        steps += [functools.partial(hidden, *p) for p in places[half:]]
        steps.append(functools.partial(product, edges // 2, edges))
        steps += [functools.partial(collect, *p) for p in places]
        done = 0
        for n, step in enumerate(steps):
            step()
            upto = (n + 1) * len(side) // len(steps)
            for s in side[done:upto]:
                s()
            done = upto

    def mix(a, b):
        tagged = [((n + 0.5) / len(a), 0, n, s) for n, s in enumerate(a)]
        tagged += [((n + 0.5) / len(b), 1, n, s) for n, s in enumerate(b)]
        return [t[3] for t in sorted(tagged, key=lambda t: t[:3])]

    def mesh_step(i, tab, idx, extra):
        gats, hids, mlps = (gat_a, gat_b), (hid_a, hid_b), (mlp_a, mlp_b)

        def fetch(b):
            if b == BLOCKS:
                return []
            return gather(tab, idx, gats[b % 2], K, R, lambda r, k: (b * R + r, k))

        for s in fetch(0):
            s()
        for b in range(BLOCKS):
            p = b % 2
            side = fetch(b + 1)
            if b in extra:
                side = mix(side, extra[b])
            messages(i, gats[p], hids[p], mlps[p], K, R, base, b * R, aggb, side)

    def halo_copies(src, rim, s_sem, r_sem):
        return [
            pltpu.make_async_remote_copy(
                src_ref=src, dst_ref=rim.at[(1 - dx) * 3 + 1 - dy],
                send_sem=s_sem.at[(1 - dx) * 3 + 1 - dy], recv_sem=r_sem.at[(1 - dx) * 3 + 1 - dy],
                device_id=at(dx, dy), device_id_type=MESH,
            )
            for dx, dy in ring
        ]

    def coarse_copy(j):
        to = (chip + j) & (CHIPS - 1)
        return pltpu.make_async_remote_copy(
            src_ref=send2.at[0 : 4 * CM], dst_ref=coarse.at[core, chip], send_sem=sc_sem, recv_sem=rc_sem,
            device_id=(lax.shift_right_logical(to, log2(NY // 2)), (to & (NY // 2 - 1)) * 2 + core),
            device_id_type=MESH,
        )

    def coarse_all():
        return pltpu.make_async_remote_copy(
            src_ref=coarse.at[core, 0 : CHIPS - 1], dst_ref=coarse.at[core, 0 : CHIPS - 1],
            send_sem=sc_sem, recv_sem=rc_sem, device_id=at(0, 1), device_id_type=MESH,
        )

    def send_rows(lo, hi, tab, new, w, send, starts):
        def project():
            spread(tab, OWN + lo, hi - lo, dot(new[lo:hi, :], w) * 0.5)

        def pack():
            send[lo * 4 : hi * 4, :] = tab[(OWN + lo) * 4 : (OWN + hi) * 4, :].astype(BF16)

        def start():
            for c in starts():
                c.start()

        return [project, pack, start]

    mesh_step(0, tab1, idx1, {
        1: update(1, pl.ds(0, R), mesh_v, aggb, nodebase, enc_v)
        + send_rows(0, R, tab2, enc_v, w_v[2, 0], send2, lambda: [coarse_copy(j) for j in range(1, CHIPS)]),
        2: update(1, pl.ds(R, R), mesh_v, aggb, nodebase, enc_v)
        + send_rows(R, MB, tab2, enc_v, w_v[2, 0], send2, lambda: halo_copies(send2, rim2, s2_sem, r2_sem)),
    })
    for s in update(1, pl.ds(MB, M - MB), mesh_v, aggb, nodebase, enc_v):
        s()

    coarse_all().wait_recv()
    forward = pltpu.make_async_remote_copy(
        src_ref=coarse.at[core], dst_ref=coarse.at[core], send_sem=sf_sem, recv_sem=rf_sem,
        device_id=(px, py ^ 1), device_id_type=MESH,
    )
    forward.start()
    spread(tab2, OWN + MB, M - MB, dot(enc_v[MB:M, :], w_v[2, 0]) * 0.5)
    base[...] = (dot(enc_v[...], w_v[2, 1]) + bias(2)) * 0.5
    nodebase[...] = dot(enc_v[...], w_v[3, 0]) + bias(3)
    copies = halo_copies(send2, rim2, s2_sem, r2_sem)
    for c in copies:
        c.wait_recv()
    unpack(tab2, RIM2, rim2, (0, 1, 2, 3, 5, 6, 7, 8), MB)
    forward.wait_recv()
    for a in range(2):
        lo = (COARSE + a * CHIPS * CM) * 4
        tab2[lo : lo + CHIPS * CM * 4, :] = coarse[a].reshape(CHIPS * CM * 4, 128).astype(F32)
    for c in copies:
        c.wait_send()
    coarse_all().wait_send()
    forward.wait_send()

    mesh_step(2, tab2, idx2, {
        2: update(3, pl.ds(0, MB), enc_v, aggb, nodebase, prc_v)
        + send_rows(0, MB, tab3, prc_v, w_v[4, 0], send3, lambda: halo_copies(send3, rim3, s3_sem, r3_sem)),
    })
    for s in update(3, pl.ds(MB, M - MB), enc_v, aggb, nodebase, prc_v):
        s()
    put_mesh = pltpu.make_async_copy(prc_v, out_mesh, out_sem.at[0])
    put_mesh.start()

    spread(tab3, OWN + MB, M - MB, dot(prc_v[MB:M, :], w_v[4, 0]) * 0.5)
    copies = halo_copies(send3, rim3, s3_sem, r3_sem)
    for c in copies:
        c.wait_recv()
    unpack(tab3, RIM2, rim3, (0, 1, 2, 3, 5, 6, 7, 8), MB)
    for c in copies:
        c.wait_send()

    def fetch3(b):
        if b == BLOCKS3:
            return []
        return gather(tab3, idx3, (gat_a, gat_b)[b % 2], K3, R3, lambda r, k: (8 * b + k, r))

    puts = []
    for s in fetch3(0):
        s()
    for b in range(BLOCKS3):
        side = fetch3(b + 1)
        if b > 0:
            done = update(5, pl.ds((b - 1) * R3, R3), grid_v, aggb3, nodebase3, dec_v)
            side = mix(side, done) if side else done
        messages(
            4, (gat_a, gat_b)[b % 2], (hid_a, hid_b)[b % 2], (mlp_a, mlp_b)[b % 2],
            K3, R3, base3, b * R3, aggb3, side,
        )
    put_grid = [
        pltpu.make_async_copy(dec_v.at[lo:hi], out_grid.at[lo:hi], out_sem.at[1 + n])
        for n, (lo, hi) in enumerate(((0, G - R3), (G - R3, G)))
    ]
    put_grid[0].start()
    for s in update(5, pl.ds(G - R3, R3), grid_v, aggb3, nodebase3, dec_v):
        s()
    put_grid[1].start()
    put_mesh.wait()
    for c in put_grid:
        c.wait()


def per_device(*args):
    any_space = pl.BlockSpec(memory_space=pl.ANY)
    dma = pltpu.SemaphoreType.DMA
    regular = pltpu.SemaphoreType.REGULAR
    vm = pltpu.VMEM
    sm = pltpu.SMEM
    i32 = jnp.int32
    return pl.pallas_call(
        kernel,
        out_shape=(jax.ShapeDtypeStruct((G, D), BF16), jax.ShapeDtypeStruct((M, D), BF16)),
        in_specs=[any_space] * len(args),
        out_specs=(any_space, any_space),
        scratch_shapes=[
            vm((G, D), BF16), vm((M, D), BF16), vm((K, M), i32), vm((K, M), i32), vm((K3, G), i32),
            vm((6, 3, D, D), BF16), vm((6, 2, D), F32),
            vm((M, 128), i32), vm((M, 128), i32), vm((BLOCKS3 * 8, 128), i32),
            sm((M, 128), i32), sm((M, 128), i32), sm((BLOCKS3 * 8, 128), i32),
            vm((ROWS1 * 4 + 8, 128), F32), vm((ROWS2 * 4 + 8, 128), F32), vm((ROWS3 * 4 + 8, 128), F32),
            vm((M, D), F32), vm((M, D), F32), vm((G, D), F32), vm((G, D), F32),
            vm((E * 4, 128), F32), vm((E * 4, 128), F32),
            vm((E, D), BF16), vm((E, D), BF16), vm((E, D), F32), vm((E, D), F32),
            vm((M, D), BF16), vm((M, D), BF16), vm((M, D), BF16), vm((G, D), BF16), vm((G, D), BF16),
            vm((GB * 4, 128), BF16), vm((9, GB * 4, 128), BF16),
            vm((MB * 4, 128), BF16), vm((9, MB * 4, 128), BF16),
            vm((2, CHIPS, CM * 4, 128), BF16),
            vm((MB * 4, 128), BF16), vm((9, MB * 4, 128), BF16),
            dma((12,)), dma((7,)), dma((3,)), dma((3,)),
            dma((9, 2)), dma((9, 2)), dma((9,)), dma((9,)), dma((9,)), dma((9,)),
            dma, dma, dma, dma,
            regular, regular,
        ],
        compiler_params=pltpu.CompilerParams(
            collective_id=0, has_side_effects=True, vmem_limit_bytes=60 * 1024 * 1024
        ),
    )(*args)


def solution(mesh):
    assert dict(mesh.shape) == {"gx": NX, "gy": NY}
    split = P(("gx", "gy"), None)
    lists = P(None, ("gx", "gy"))
    return jax.shard_map(
        per_device,
        mesh=mesh,
        in_specs=(split, split, lists, lists, lists) + (P(),) * 12,
        out_specs=(split, split),
        check_vma=False,
    )
```

time: 62.4 us -> 45.4 us (0.73); the launches traced: 61.5 us -> 45.2 us
  Pallas kernels: 57.4 us -> 41.1 us
    pallas_call x1, Pallas kernels: 57.4 us -> 41.1 us  [per_device(): pl.pallas_call(kernel, out_shape=(jax.ShapeDtypeStruct((G, D), BF16), jax...]
where the time goes in v2:
time: 45.4 us; the launch traced here: 45.2 us
  Pallas kernels  41.1 us (91%)
  local copies, waits for them, and re-layouts  3.44 us (8%)
  between operations  0.65 us (1%)
    pallas_call x1, Pallas kernels, per_device(): pl.pallas_call(kernel, out_shape=(jax.ShapeDtypeStruct((G, D), BF16), jax...  41.1 us
    unnamed x2, local copies, waits for them, and re-layouts  3.44 us

profile of v2, /device:TPU:0, one launch (start us, length us, event | category | flops | bytes accessed | tf_op | source)
XLA Modules:
  0.0 45.2 jit_solution(12835206027521426047)
XLA Ops:
  0.6 41.1 %shard_map.176 = (bf16[512,512]{1,0:T(8,128)(2,1)}, bf16[128,512]{1,0:T(8,128)(2,1)}) custom-call(bf16[512,512]{1,0:T(8,128)(2,1)} %grid.1, bf16[128,512]{1,0:T(8,128)(2,1)} %mesh.1, s32[32,128]{1,0:T(8,128)} %encs.1, s32[32,128]{1,0:T(8,128)} %mshs.1, s32[3,512]{1,0:T(4,128)} %decs.1, bf16[3,512,512]{2,1,0:T(8,128)(2,1)} %w0.1, f32[2,512]{1,0:T(2,128)} %v0.1, ...), custom_call_target="tpu_custom_call" | custom-call | tf_op jit(solution)/shard_map/pallas_call | solution.py:463
  41.8 1.9 %copy.21 = bf16[512,512]{1,0:T(8,128)(2,1)} copy(bf16[512,512]{1,0:T(8,128)(2,1)} %get-tuple-element.4) | data formatting | bytes 1048576
  43.7 1.6 %copy.22 = bf16[128,512]{1,0:T(8,128)(2,1)} copy(bf16[128,512]{1,0:T(8,128)(2,1)} %get-tuple-element.5) | data formatting | bytes 262144

commit v3 on v2

--- a/solution.py
+++ b/solution.py
@@ -55,7 +55,7 @@
     dx = (ox - px) & (NX - 1)
     dy = (oy - py) & (NY - 1)
     sx = jnp.where(dx == 1, 2, jnp.where(dx == NX - 1, 0, 1))
-    sy = jnp.where(dy == 1, 2, jnp.where(dy == NY - 1, 0, 1))
+    sy = jnp.where(dy == 0, 1, jnp.where(oy == (py ^ 1), 2, 0))
     near = ((dx <= 1) | (dx == NX - 1)) & ((dy <= 1) | (dy == NY - 1)) & (off < border)
     itself = (dx == 0) & (dy == 0)
     place = (owner & 1) * CHIPS + lax.shift_right_arithmetic(owner, 1)
@@ -109,11 +109,11 @@
     wloads = {0: pltpu.make_async_copy(w0.at[1:3], w_v.at[0, 1:3], w_sem.at[6])}
     for i, s in enumerate((w1, w2, w3, w4, w5)):
         wloads[i + 1] = pltpu.make_async_copy(s, w_v.at[i + 1], w_sem.at[i + 1])
-    border_load.start()
-    first_weight.start()
     barrier = pltpu.get_barrier_semaphore()
     for p in partners:
         pl.semaphore_signal(barrier, inc=1, device_id=p, device_id_type=MESH)
+    border_load.start()
+    first_weight.start()
     for c in loads:
         c.start()
     wloads[0].start()
@@ -139,6 +139,9 @@
             return carry
 
         lax.fori_loop(0, D // 128, some, 0)
+
+    across = 1 - 2 * (1 - core)
+    sides = {0: at(0, across), 2: at(0, -across)}
 
     def border_copy(src, sx, sy, to, half):
         slot = sx * 3 + sy
@@ -148,21 +151,19 @@
             device_id=to, device_id_type=MESH,
         )
 
+    def kept_half(slot, half):
+        return rim1.at[slot, half * HALF : half * HALF + HALF]
+
     border_load.wait()
     first_weight.wait()
     spread(tab1, OWN, GB, dot(grid_v[0:GB, :], w_v[0, 0]) * 0.5)
     send1[...] = tab1[OWN * 4 : (OWN + GB) * 4, :].astype(BF16)
     pl.semaphore_wait(barrier, len(partners))
-    along_x = [[], []]
-    along_y = [[], []]
-    for half in range(2):
-        part = send1.at[half * HALF : half * HALF + HALF]
-        for d in (1, -1):
-            along_x[half].append(border_copy(part, 1 - d, 1, at(d, 0), half))
-            along_y[half].append(border_copy(part, 1, 1 - d, at(0, d), half))
-    for half in range(2):
-        for c in along_x[half] + along_y[half]:
-            c.start()
+    halves = [send1.at[h * HALF : h * HALF + HALF] for h in range(2)]
+    along_x = [[border_copy(halves[h], 1 - d, 1, at(d, 0), h) for d in (1, -1)] for h in range(2)]
+    aside = {(sy, h): border_copy(halves[h], 1, sy, sides[sy], h) for sy in (0, 2) for h in range(2)}
+    for c in along_x[0] + [aside[0, 1]] + along_x[1] + [aside[0, 0], aside[2, 0], aside[2, 1]]:
+        c.start()
     for i in (1, 4, 5, 2, 3):
         wloads[i].start()
     for p in lines:
@@ -192,29 +193,29 @@
     idx_loads[0].start()
     wloads[0].wait()
     base[...] = (dot(mesh_v[...], w_v[0, 1]) + bias(0)) * 0.5
-    pl.semaphore_wait(meet_a, len(lines))
-    for p in lines:
-        pl.semaphore_signal(meet_b, inc=1, device_id=p, device_id_type=MESH)
-
-    corners = [[], []]
-    for half in range(2):
-        for sx in (0, 2):
-            part = rim1.at[sx * 3 + 1, half * HALF : half * HALF + HALF]
-            for d in (1, -1):
-                corners[half].append(border_copy(part, sx, 1 - d, at(0, d), half))
+
+    to_core = [[border_copy(kept_half(sx * 3 + 1, h), sx, 2, sides[2], h) for sx in (0, 2)] for h in range(2)]
+    to_chip = [border_copy(kept_half(sx * 3 + 1, 0), sx, 0, sides[0], 0) for sx in (0, 2)]
+    to_x = [border_copy(kept_half(3, 1), 1 - d, 0, at(d, 0), 1) for d in (1, -1)]
 
     for c in along_x[0]:
         c.wait_recv()
-    for c in corners[0]:
+    for c in to_chip + to_core[0]:
         c.start()
     centre(0)
     wloads[1].wait()
     centre(1)
     nodebase[...] = dot(mesh_v[...], w_v[1, 0]) + bias(1)
+    aside[0, 1].wait_recv()
+    for c in to_x:
+        c.start()
     for c in along_x[1]:
         c.wait_recv()
-    for c in corners[1]:
+    for c in to_core[1]:
         c.start()
+    pl.semaphore_wait(meet_a, len(lines))
+    for p in lines:
+        pl.semaphore_signal(meet_b, inc=1, device_id=p, device_id_type=MESH)
     place(mshs_v, pos2, M, MB, RIM2)
     pos3[...] = jnp.zeros(pos3.shape, jnp.int32)
     for b in range(BLOCKS3):
@@ -235,18 +236,14 @@
             tab[lo : lo + rows * 4, :] = rim[slot].astype(F32)
 
     unpack(tab1, RIM1, rim1, (1, 7), GB)
-    for c in along_y[0] + along_y[1]:
+    for c in to_core[0] + to_core[1] + [aside[0, 0], aside[2, 0], aside[2, 1]]:
         c.wait_recv()
-    unpack(tab1, RIM1, rim1, (3, 5), GB)
-    for c in corners[0] + corners[1]:
+    unpack(tab1, RIM1, rim1, (3, 5, 2, 8), GB)
+    for c in to_chip + to_x:
         c.wait_recv()
-    unpack(tab1, RIM1, rim1, (0, 2, 6, 8), GB)
-    for half in range(2):
-        for c in along_x[half] + along_y[half] + corners[half]:
-            c.wait_send()
+    unpack(tab1, RIM1, rim1, (0, 6), GB)
     for c in idx_loads:
         c.wait()
-    pl.semaphore_wait(meet_b, len(lines))
 
     def update(i, rows, x, agg, node, new):
         kept = {}
@@ -339,14 +336,16 @@
             messages(i, gats[p], hids[p], mlps[p], K, R, base, b * R, aggb, side)
 
     def halo_copies(src, rim, s_sem, r_sem):
-        return [
-            pltpu.make_async_remote_copy(
-                src_ref=src, dst_ref=rim.at[(1 - dx) * 3 + 1 - dy],
-                send_sem=s_sem.at[(1 - dx) * 3 + 1 - dy], recv_sem=r_sem.at[(1 - dx) * 3 + 1 - dy],
-                device_id=at(dx, dy), device_id_type=MESH,
+        copies = []
+        for dx, sy in ((1, 0), (-1, 0), (0, 0), (1, 1), (-1, 1), (1, 2), (-1, 2), (0, 2)):
+            slot = (1 - dx) * 3 + sy
+            copies.append(
+                pltpu.make_async_remote_copy(
+                    src_ref=src, dst_ref=rim.at[slot], send_sem=s_sem.at[slot], recv_sem=r_sem.at[slot],
+                    device_id=at(dx, (0 if sy == 1 else across if sy == 0 else -across)), device_id_type=MESH,
+                )
             )
-            for dx, dy in ring
-        ]
+        return copies
 
     def coarse_copy(j):
         to = (chip + j) & (CHIPS - 1)
@@ -362,6 +361,10 @@
             send_sem=sc_sem, recv_sem=rc_sem, device_id=at(0, 1), device_id_type=MESH,
         )
 
+    def all_coarse():
+        pl.semaphore_wait(meet_b, len(lines))
+        return [coarse_copy(j) for j in range(1, CHIPS)]
+
     def send_rows(lo, hi, tab, new, w, send, starts):
         def project():
             spread(tab, OWN + lo, hi - lo, dot(new[lo:hi, :], w) * 0.5)
@@ -377,12 +380,15 @@
 
     mesh_step(0, tab1, idx1, {
         1: update(1, pl.ds(0, R), mesh_v, aggb, nodebase, enc_v)
-        + send_rows(0, R, tab2, enc_v, w_v[2, 0], send2, lambda: [coarse_copy(j) for j in range(1, CHIPS)]),
+        + send_rows(0, R, tab2, enc_v, w_v[2, 0], send2, all_coarse),
         2: update(1, pl.ds(R, R), mesh_v, aggb, nodebase, enc_v)
         + send_rows(R, MB, tab2, enc_v, w_v[2, 0], send2, lambda: halo_copies(send2, rim2, s2_sem, r2_sem)),
     })
     for s in update(1, pl.ds(MB, M - MB), mesh_v, aggb, nodebase, enc_v):
         s()
+
+    for c in along_x[0] + along_x[1] + list(aside.values()) + to_core[0] + to_core[1] + to_chip + to_x:
+        c.wait_send()
 
     coarse_all().wait_recv()
     forward = pltpu.make_async_remote_copy(

time: 45.4 us -> 45.1 us (level)
  no operation moved by 1% of the time
where the time goes in v3:
time: 45.1 us; the launch traced here: 44.8 us
  Pallas kernels  40.7 us (90%)
  local copies, waits for them, and re-layouts  3.44 us (8%)
  between operations  0.65 us (1%)
    pallas_call x1, Pallas kernels, per_device(): pl.pallas_call(kernel, out_shape=(jax.ShapeDtypeStruct((G, D), BF16), jax...  40.7 us
    unnamed x2, local copies, waits for them, and re-layouts  3.44 us

profile of v3, /device:TPU:0, one launch (start us, length us, event | category | flops | bytes accessed | tf_op | source)
XLA Modules:
  0.0 44.8 jit_solution(14147958565386835120)
XLA Ops:
  0.6 40.7 %shard_map.176 = (bf16[512,512]{1,0:T(8,128)(2,1)}, bf16[128,512]{1,0:T(8,128)(2,1)}) custom-call(bf16[512,512]{1,0:T(8,128)(2,1)} %grid.1, bf16[128,512]{1,0:T(8,128)(2,1)} %mesh.1, s32[32,128]{1,0:T(8,128)} %encs.1, s32[32,128]{1,0:T(8,128)} %mshs.1, s32[3,512]{1,0:T(4,128)} %decs.1, bf16[3,512,512]{2,1,0:T(8,128)(2,1)} %w0.1, f32[2,512]{1,0:T(2,128)} %v0.1, ...), custom_call_target="tpu_custom_call" | custom-call | tf_op jit(solution)/shard_map/pallas_call | solution.py:469
  41.4 1.9 %copy.21 = bf16[512,512]{1,0:T(8,128)(2,1)} copy(bf16[512,512]{1,0:T(8,128)(2,1)} %get-tuple-element.4) | data formatting | bytes 1048576
  43.2 1.6 %copy.22 = bf16[128,512]{1,0:T(8,128)(2,1)} copy(bf16[128,512]{1,0:T(8,128)(2,1)} %get-tuple-element.5) | data formatting | bytes 262144

commit v4 on v3

--- a/solution.py
+++ b/solution.py
@@ -280,11 +280,15 @@
         places = [(first, k) for first in range(0, receivers, 16) for k in range(slots)]
         half = len(places) // 2
 
+        bases = {}
+
         def hidden(first, k):
             e = first * slots + k * 16
+            if k == 0:
+                bases[first] = base_ref[base_row + first : base_row + first + 16, :]
             for c in range(4):
                 cols = slice(128 * c, 128 * c + 128)
-                y = gat[pl.ds(4 * e + c, 16, stride=4), :] + base_ref[base_row + first : base_row + first + 16, cols]
+                y = gat[pl.ds(4 * e + c, 16, stride=4), :] + bases[first][:, cols]
                 hid[e : e + 16, cols] = silu_half(y).astype(BF16)
 
         def product(lo, hi):
@@ -459,6 +463,19 @@
         c.wait()
 
 
+def hand_on(grid, mesh, out_grid, out_mesh, grid_v, mesh_v, sem):
+    pieces = [(grid, grid_v, out_grid), (mesh, mesh_v, out_mesh)]
+    takes = [pltpu.make_async_copy(a, b, sem.at[n]) for n, (a, b, _) in enumerate(pieces)]
+    gives = [pltpu.make_async_copy(b, c, sem.at[2 + n]) for n, (_, b, c) in enumerate(pieces)]
+    for c in takes:
+        c.start()
+    for a, b in ((takes[1], gives[1]), (takes[0], gives[0])):
+        a.wait()
+        b.start()
+    for c in gives:
+        c.wait()
+
+
 def per_device(*args):
     any_space = pl.BlockSpec(memory_space=pl.ANY)
     dma = pltpu.SemaphoreType.DMA
@@ -466,9 +483,10 @@
     vm = pltpu.VMEM
     sm = pltpu.SMEM
     i32 = jnp.int32
-    return pl.pallas_call(
+    shapes = (jax.ShapeDtypeStruct((G, D), BF16), jax.ShapeDtypeStruct((M, D), BF16))
+    results = pl.pallas_call(
         kernel,
-        out_shape=(jax.ShapeDtypeStruct((G, D), BF16), jax.ShapeDtypeStruct((M, D), BF16)),
+        out_shape=shapes,
         in_specs=[any_space] * len(args),
         out_specs=(any_space, any_space),
         scratch_shapes=[
@@ -494,6 +512,14 @@
             collective_id=0, has_side_effects=True, vmem_limit_bytes=60 * 1024 * 1024
         ),
     )(*args)
+    return pl.pallas_call(
+        hand_on,
+        out_shape=shapes,
+        in_specs=[any_space] * 2,
+        out_specs=(any_space, any_space),
+        scratch_shapes=[vm((G, D), BF16), vm((M, D), BF16), dma((4,))],
+        compiler_params=pltpu.CompilerParams(vmem_limit_bytes=60 * 1024 * 1024),
+    )(*results)
 
 
 def solution(mesh):

time: 45.1 us -> 43.7 us (0.969)
  local copies, waits for them, and re-layouts: 3.44 us -> 0 us
  Pallas kernels: 40.7 us -> 42.7 us
    unnamed x2 -> x0, local copies, waits for them, and re-layouts: 3.44 us -> none
    pallas_call x1 -> x2, Pallas kernels: 40.7 us -> 42.7 us  [the longest x1 40.7 us: per_device(): pl.pallas_call(kernel, out_shape=shapes, in_specs=[any_space] * len(args)...]
where the time goes in v4:
time: 43.7 us; the launch traced here: 43.5 us
  Pallas kernels  42.7 us (98%)
  between operations  0.81 us (2%)
    pallas_call x1, Pallas kernels, per_device(): pl.pallas_call(kernel, out_shape=shapes, in_specs=[any_space] * len(args)...  40.7 us
    pallas_call x1, Pallas kernels, per_device(): pl.pallas_call(hand_on, out_shape=shapes, in_specs=[any_space] * 2, out_s...  1.93 us

profile of v4, /device:TPU:0, one launch (start us, length us, event | category | flops | bytes accessed | tf_op | source)
XLA Modules:
  0.0 43.5 jit_solution(10001023511498781995)
XLA Ops:
  0.6 40.7 %shard_map.176 = (bf16[512,512]{1,0:T(8,128)(2,1)}, bf16[128,512]{1,0:T(8,128)(2,1)}) custom-call(bf16[512,512]{1,0:T(8,128)(2,1)} %grid.1, bf16[128,512]{1,0:T(8,128)(2,1)} %mesh.1, s32[32,128]{1,0:T(8,128)} %encs.1, s32[32,128]{1,0:T(8,128)} %mshs.1, s32[3,512]{1,0:T(4,128)} %decs.1, bf16[3,512,512]{2,1,0:T(8,128)(2,1)} %w0.1, f32[2,512]{1,0:T(2,128)} %v0.1, ...), custom_call_target="tpu_custom_call" | custom-call | tf_op jit(solution)/shard_map/pallas_call | solution.py:487
  41.4 1.9 %shard_map.177 = (bf16[512,512]{1,0:T(8,128)(2,1)}, bf16[128,512]{1,0:T(8,128)(2,1)}) custom-call(bf16[512,512]{1,0:T(8,128)(2,1)} %get-tuple-element.4.grid, bf16[128,512]{1,0:T(8,128)(2,1)} %get-tuple-element.5.mesh), custom_call_target="tpu_custom_call" | custom-call | tf_op jit(solution)/shard_map/pallas_call | solution.py:515
